TPU v7x, 32 devices: a whole 2x2x4 slice. The times are simulated.
32 devices in a mesh: slab: 16 (over z, y, x), cell: 2 (over core).
Axes of the slice: x: 2, y: 2, z: 4, core: 2. Of those that a mesh axis runs over, the one named last changes fastest.
Arguments:
- cell_row: int32 [16384], P(('slab', 'cell')), may hold values from 0 to 2043, as said below
- cell_col: int32 [16384], P(('slab', 'cell')), may hold values from 0 to 2039
- cell_width: int32 [16384], P(('slab', 'cell')), may hold values from 1 to 8
- cell_height: int32 [16384], P(('slab', 'cell')), may hold values from 1 to 4
- cell_region: int32 [16384], P(('slab', 'cell')), may hold values from 0 to 3
- cell_offset: float32 [2, 16384], P(None, ('slab', 'cell')), may hold values from 0 to 1
Outputs:
- field_x: float32 [4, 2048, 2048], P(None, ('slab', 'cell'))
- field_y: float32 [4, 2048, 2048], P(None, ('slab', 'cell'))
- cell_force: float32 [2, 16384], P(None, ('slab', 'cell'))
- energy: float32 [], replicated
- overflow: float32 [], replicated
Inputs may be any that keep to these rules, and one draw needn't show every extreme that they name: `cell_row`: cell i belongs to row slab s = i // 1024: its row lies in [s * 128, (s + 1) * 128); cells of the last slab lie at least 4 rows below the top of the grid.
All inputs are finite; a program needn't handle non-finite values.
Results may differ from a plain program's by a relative error of at most 0.0015.
Values may be sent and summed in bfloat16 or wider, within the bound.
No kernel may reach another device: no remote copies, remote signals or barrier semaphores. Data moves between devices by JAX's collectives and lax.ppermute only.
A program may use at most 128 MiB of HBM per device.

v0:
```python
import functools
import math

import jax
import jax.numpy as jnp
import numpy as np
from jax import lax
from jax.experimental import pallas as pl
from jax.experimental.pallas import tpu as pltpu
from jax.sharding import PartitionSpec as P

M = 2048
REGIONS = 4
HMAX = 4
WMAX = 8
HALF = M // 2
STRIP = 32
BAND = 4
TILE = 256
PARTS = HALF // TILE
FINE = 8192.0
AXES = ("slab", "cell")
BF = jnp.bfloat16
F32 = jnp.float32
I16 = jnp.int16
VMEM_LIMIT = 56 * 1024 * 1024


def params():
    return pltpu.CompilerParams(
        dimension_semantics=("arbitrary",), vmem_limit_bytes=VMEM_LIMIT
    )


def steps_of(bound):
    return 32700.0 / math.log2(1.0 + bound * FINE)


def encode_wide(value, steps):
    code = jnp.minimum(jnp.log2(1.0 + jnp.abs(value) * FINE) * steps, 32767.0)
    return jnp.round(jnp.where(value < 0.0, -code, code))


def encode(value, steps):
    return encode_wide(value, steps).astype(jnp.int32).astype(I16)


def packable(rows):
    return rows == 64 and REGIONS == 4


def swap_halves(values):
    lane = lax.broadcasted_iota(jnp.int32, values[0].shape, 1)
    turned = [pltpu.roll(value, 64, 1) for value in values]
    first = jnp.where(lane < 64, values[0], turned[1])
    second = jnp.where(lane < 64, turned[0], values[1])
    return first, second


def pack(out, value):
    for pair in range(TILE // 128):
        tile = value[:, pair * 128 : (pair + 1) * 128]
        for half in range(2):
            here = pl.ds(half * 128, 128)
            low = tile[half * 128 : half * 128 + 64]
            high = tile[half * 128 + 64 : half * 128 + 128]
            first, second = swap_halves((low, high))
            out[2 * pair, :, here] = first.astype(jnp.int32).astype(I16)
            out[2 * pair + 1, :, here] = second.astype(jnp.int32).astype(I16)


def decode(code, steps):
    wide = code.astype(jnp.int32).astype(F32)
    size = (jnp.exp2(jnp.abs(wide) * (1.0 / steps)) - 1.0) * (1.0 / FINE)
    return jnp.where(wide < 0.0, -size, size)


def split(value):
    high = value.astype(BF)
    return high, (value - high.astype(F32)).astype(BF)


def dot(left, right):
    return lax.dot_general(left, right, (((1,), (0,)), ((), ())), preferred_element_type=F32)


def dot3(left_hi, left_lo, right_hi, right_lo):
    return dot(left_hi, right_hi) + (dot(left_lo, right_hi) + dot(left_hi, right_lo))


def base_tables():
    groups = HALF // STRIP
    unit = math.pi / (2 * M)
    turn = 4 * M
    place = (2 * np.arange(HALF) + 1)[None, :]
    freq = (2 * np.arange(HALF))[None, :]
    group = np.arange(groups)[:, None]
    inside = np.arange(STRIP)[:, None]
    gain = math.sqrt(2.0 / M)
    zero_gain = np.where(freq == 0, math.sqrt(0.5), 1.0)
    far = unit * (2 * STRIP * group * place % turn)
    far_t = unit * (2 * STRIP * group * freq % turn)
    near_even = unit * (2 * inside * place % turn)
    near_odd = unit * ((2 * inside + 1) * place % turn)
    near_t = unit * ((2 * inside + 1) * freq % turn)
    outer = np.stack([np.cos(far), np.sin(far), np.cos(far_t), np.sin(far_t)], axis=1)
    inner = np.stack(
        [
            gain * np.cos(near_even),
            gain * np.sin(near_even),
            gain * np.cos(near_odd),
            gain * np.sin(near_odd),
            gain * zero_gain * np.cos(near_t),
            gain * zero_gain * np.sin(near_t),
        ]
    )
    return outer.astype(np.float32), inner.astype(np.float32)


def table_kernel(outer, inner, fwd_hi, fwd_lo, sy_hi, sy_lo, ce_hi, ce_lo, se_hi, se_lo):
    for group in range(BAND):
        here = pl.ds(group * STRIP, STRIP)

        def pair(far, near):
            cos_far = outer[group, far : far + 1, :]
            sin_far = outer[group, far + 1 : far + 2, :]
            cos_near = inner[near]
            sin_near = inner[near + 1]
            return cos_far * cos_near - sin_far * sin_near, sin_far * cos_near + cos_far * sin_near

        cos_even, sin_even = pair(0, 0)
        if group == 0:
            row = lax.broadcasted_iota(jnp.int32, (STRIP, 1), 0) + pl.program_id(0) * STRIP
            cos_even = cos_even * jnp.where(row == 0, math.sqrt(0.5), 1.0).astype(F32)
        ce_hi[here, :], ce_lo[here, :] = split(cos_even)
        se_hi[here, :], se_lo[here, :] = split(sin_even)
        cos_odd, sin_odd = pair(0, 2)
        fwd_hi[here, HALF:], fwd_lo[here, HALF:] = split(cos_odd)
        sy_hi[here, HALF:], sy_lo[here, HALF:] = split(sin_odd)
        cos_t, sin_t = pair(2, 4)
        fwd_hi[here, :HALF], fwd_lo[here, :HALF] = split(cos_t)
        sy_hi[here, :HALF], sy_lo[here, :HALF] = split(sin_t)


def make_tables():
    outer, inner = base_tables()
    wide = jax.ShapeDtypeStruct((HALF, M), BF)
    square = jax.ShapeDtypeStruct((HALF, HALF), BF)
    wide_spec = pl.BlockSpec((BAND * STRIP, M), lambda g: (g, 0))
    square_spec = pl.BlockSpec((BAND * STRIP, HALF), lambda g: (g, 0))
    return pl.pallas_call(
        table_kernel,
        grid=(HALF // (BAND * STRIP),),
        in_specs=[
            pl.BlockSpec((BAND, 4, HALF), lambda g: (g, 0, 0)),
            pl.BlockSpec((6, STRIP, HALF), lambda g: (0, 0, 0)),
        ],
        out_specs=[wide_spec] * 4 + [square_spec] * 4,
        out_shape=[wide] * 4 + [square] * 4,
        compiler_params=params(),
        cost_estimate=pl.CostEstimate(
            flops=40 * HALF * HALF, transcendentals=0, bytes_accessed=24 * HALF * HALF
        ),
        name="tables",
    )(jnp.asarray(outer), jnp.asarray(inner))


def fold_rows(value):
    rows, cols = value.shape
    folded = jnp.sum(value.reshape(rows // 8, 8, cols), axis=0)
    out = folded[:, :128]
    for start in range(128, cols, 128):
        out = out + folded[:, start : start + 128]
    return out


def density_kernel(
    device,
    cells,
    fwd_hi,
    fwd_lo,
    xt,
    yt,
    codes,
    sums,
    dens,
    part_hi,
    part_lo,
    *,
    steps,
    rows,
    count,
):
    step = pl.program_id(0)
    total = cells.shape[1]
    chunk = 512

    @pl.when(step == 0)
    def _():
        line = lax.broadcasted_iota(jnp.int32, (yt.shape[0], 1), 0)
        inside = line & (rows - 1)
        place = jnp.where(device[0] >= count // 2, rows - 1 - inside, inside) + device[0] * rows
        place = place.astype(F32)
        region = (line >> (rows.bit_length() - 1)).astype(F32)
        for start in range(0, total, chunk):
            here = pl.ds(start, chunk)
            low = cells[6:7, here]
            rel = place - cells[0:1, here]
            high = jnp.minimum(rel + 1.0, low + cells[3:4, here])
            value = jnp.maximum(high - jnp.maximum(rel, low), 0.0)
            yt[:, here] = jnp.where(region == cells[4:5, here], value, 0.0).astype(BF)

    @pl.when(step < 2 * PARTS)
    def _():
        place = (step % PARTS) * TILE + lax.broadcasted_iota(jnp.int32, (TILE, 1), 0)
        place = jnp.where(step >= PARTS, M - 1 - place, place).astype(F32)
        acc = None
        for start in range(0, total, chunk):
            here = pl.ds(start, chunk)
            low = cells[5:6, here]
            rel = place - cells[1:2, here]
            high = jnp.minimum(rel + 1.0, low + cells[2:3, here])
            value = jnp.maximum(high - jnp.maximum(rel, low), 0.0).astype(BF)
            xt[:, here] = value
            part = lax.dot_general(
                yt[:, here], value, (((1,), (1,)), ((), ())), preferred_element_type=F32
            )
            acc = part if acc is None else acc + part
        dens[step] = acc

    @pl.when(step == 2 * PARTS)
    def _():
        over = jnp.zeros((8, 128), F32)
        full = jnp.zeros((8, 128), F32)
        for part in range(PARTS):
            here = pl.ds(part * TILE, TILE)
            near = dens[part]
            mirrored = dens[PARTS + part]
            even = near + mirrored
            over = over + fold_rows(
                jnp.maximum(near - 1.0, 0.0) + jnp.maximum(mirrored - 1.0, 0.0)
            )
            full = full + fold_rows(even)
            part_hi[0, :, here], part_lo[0, :, here] = split(even)
            part_hi[1, :, here], part_lo[1, :, here] = split(near - mirrored)
        sums[0:8, :] = over
        sums[8:16, :] = full

    @pl.when(step >= 2 * PARTS)
    def _():
        odd = jnp.where(step >= 3 * PARTS, 1, 0)
        out = dot3(part_hi[odd], part_lo[odd], fwd_hi[...], fwd_lo[...])
        if packable(rows):
            pack(codes, encode_wide(out, steps))
        else:
            codes[...] = encode(out, steps)


def density_call(device, cells, tables, rows, count, steps):
    total = cells.shape[1]
    lines = REGIONS * rows
    late = lambda t: (0, jnp.maximum(t - 2 * PARTS, 0))
    whole = lambda t: (0, 0)
    if packable(rows):
        code_spec = pl.BlockSpec(
            (TILE // rows, rows, lines), lambda t: (jnp.maximum(t - 2 * PARTS, 0), 0, 0)
        )
        code_shape = (count, rows, lines)
    else:
        code_spec = pl.BlockSpec((lines, TILE), late)
        code_shape = (lines, M)
    return pl.pallas_call(
        functools.partial(density_kernel, steps=steps, rows=rows, count=count),
        grid=(4 * PARTS,),
        in_specs=[
            pl.BlockSpec(memory_space=pltpu.SMEM),
            pl.BlockSpec((8, total), whole),
            pl.BlockSpec((HALF, TILE), late),
            pl.BlockSpec((HALF, TILE), late),
        ],
        out_specs=[
            pl.BlockSpec((TILE, total), lambda t: (jnp.minimum(t, 2 * PARTS - 1), 0)),
            pl.BlockSpec((lines, total), whole),
            code_spec,
            pl.BlockSpec((16, 128), whole),
        ],
        out_shape=[
            jax.ShapeDtypeStruct((M, total), BF),
            jax.ShapeDtypeStruct((lines, total), BF),
            jax.ShapeDtypeStruct(code_shape, I16),
            jax.ShapeDtypeStruct((16, 128), F32),
        ],
        scratch_shapes=[
            pltpu.VMEM((2 * PARTS, lines, TILE), F32),
            pltpu.VMEM((2, lines, HALF), BF),
            pltpu.VMEM((2, lines, HALF), BF),
        ],
        compiler_params=params(),
        cost_estimate=pl.CostEstimate(
            flops=2 * lines * M * (total + 3 * HALF), transcendentals=0, bytes_accessed=1 << 24
        ),
        name="density",
    )(device, cells, tables[0], tables[1])


def place_rows(out, first, top, bottom, steps):
    count, rows = out.shape[0], out.shape[1]
    top = encode(top, steps)
    bottom = encode(bottom, steps)
    for inner in range(TILE // rows):
        here = slice(inner * rows, (inner + 1) * rows)
        out[first + inner] = top[here]
        out[count - 1 - first - inner] = bottom[here]


def spectrum_kernel(
    device,
    codes,
    ce_hi,
    ce_lo,
    co_hi,
    co_lo,
    ct_hi,
    ct_lo,
    out,
    dye_hi,
    dye_lo,
    dyo_hi,
    dyo_lo,
    energy,
    even_hi,
    even_lo,
    odd_hi,
    odd_lo,
    dxe_hi,
    dxe_lo,
    dxo_hi,
    dxo_lo,
    *,
    fwd_steps,
    back_steps,
):
    step = pl.program_id(0)
    count, rows = codes.shape[0], codes.shape[1]

    @pl.when(step == 0)
    def _():
        for block in range(count // 2):
            here = pl.ds(block * rows, rows)
            near = decode(codes[block], fwd_steps)
            mirrored = decode(codes[count - 1 - block], fwd_steps)
            even_hi[here, :], even_lo[here, :] = split(near + mirrored)
            odd_hi[here, :], odd_lo[here, :] = split(near - mirrored)
        energy[...] = jnp.zeros((8, 128), F32)

    @pl.when(step < PARTS)
    def _():
        unit = math.pi / M
        lane = lax.broadcasted_iota(jnp.int32, (1, codes.shape[2]), 1) & (rows - 1)
        odd = jnp.where(device[0] >= count // 2, 1, 0)
        q = (2 * (rows * (device[0] - odd * (count // 2)) + lane) + odd).astype(F32)
        first = lax.broadcasted_iota(jnp.int32, (TILE, 1), 0) + step * TILE
        here = pl.ds(pl.multiple_of(step * TILE, TILE), TILE)

        def solve(spectrum, p):
            squared = p * p + q * q
            inverse = jnp.where(squared == 0.0, 0.0, 1.0 / jnp.where(squared == 0.0, 1.0, squared))
            scaled = spectrum * inverse
            return scaled * (q * (1.0 / unit)), scaled * (p * (1.0 / unit)), spectrum * scaled

        spec = dot3(ce_hi[...], ce_lo[...], even_hi[...], even_lo[...])
        drive_x, drive_y, power = solve(spec, (2 * first).astype(F32))
        dxe_hi[here, :], dxe_lo[here, :] = split(drive_x)
        dye_hi[...], dye_lo[...] = split(drive_y)
        spec = dot3(co_hi[...], co_lo[...], odd_hi[...], odd_lo[...])
        drive_x, drive_y, more = solve(spec, (2 * first + 1).astype(F32))
        dxo_hi[here, :], dxo_lo[here, :] = split(drive_x)
        dyo_hi[...], dyo_lo[...] = split(drive_y)
        both = power + more
        if both.shape[1] % 128:
            both = jnp.concatenate(
                [both, jnp.zeros((TILE, 128 - both.shape[1] % 128), F32)], axis=1
            )
        energy[...] += fold_rows(both) * (1.0 / (unit * unit))

    @pl.when(step >= PARTS)
    def _():
        even = dot3(ct_hi[...], ct_lo[...], dxe_hi[...], dxe_lo[...])
        odd = dot3(co_hi[...], co_lo[...], dxo_hi[...], dxo_lo[...])
        first = (step - PARTS) * (TILE // rows)
        place_rows(out, first, even + odd, even - odd, back_steps)


def spectrum_call(device, codes, tables, fwd_steps, back_steps):
    fwd_hi, fwd_lo, _, _, ce_hi, ce_lo, _, _ = tables
    count, rows, cols = codes.shape
    early = lambda t: (jnp.minimum(t, PARTS - 1), 0)
    drive = jax.ShapeDtypeStruct((HALF, cols), BF)
    return pl.pallas_call(
        functools.partial(spectrum_kernel, fwd_steps=fwd_steps, back_steps=back_steps),
        grid=(2 * PARTS,),
        in_specs=[
            pl.BlockSpec(memory_space=pltpu.SMEM),
            pl.BlockSpec((count, rows, cols), lambda t: (0, 0, 0)),
        ]
        + [pl.BlockSpec((TILE, HALF), early)] * 2
        + [pl.BlockSpec((TILE, HALF), lambda t: (t % PARTS, 1))] * 2
        + [pl.BlockSpec((TILE, HALF), lambda t: (jnp.maximum(t - PARTS, 0), 0))] * 2,
        out_specs=[pl.BlockSpec((count, rows, cols), lambda t: (0, 0, 0))]
        + [pl.BlockSpec((TILE, cols), early)] * 4
        + [pl.BlockSpec((8, 128), lambda t: (0, 0))],
        out_shape=[jax.ShapeDtypeStruct((count, rows, cols), I16)]
        + [drive] * 4
        + [jax.ShapeDtypeStruct((8, 128), F32)],
        scratch_shapes=[pltpu.VMEM((HALF, cols), BF)] * 8,
        compiler_params=params(),
        cost_estimate=pl.CostEstimate(
            flops=24 * HALF * HALF * cols, transcendentals=0, bytes_accessed=1 << 24
        ),
        name="spectrum",
    )(device, codes, ce_hi, ce_lo, fwd_hi, fwd_lo, fwd_hi, fwd_lo)


def sine_kernel(
    dye_hi, dye_lo, dyo_hi, dyo_lo, se_hi, se_lo, so_hi, so_lo, out, *, back_steps
):
    even = dot3(se_hi[...], se_lo[...], dye_hi[...], dye_lo[...])
    odd = dot3(so_hi[...], so_lo[...], dyo_hi[...], dyo_lo[...])
    first = pl.program_id(0) * (TILE // out.shape[1])
    place_rows(out, first, odd + even, odd - even, back_steps)


def sine_call(drives, tables, count, rows, back_steps):
    sy_hi, sy_lo = tables[2], tables[3]
    cols = drives[0].shape[1]
    return pl.pallas_call(
        functools.partial(sine_kernel, back_steps=back_steps),
        grid=(PARTS,),
        in_specs=[pl.BlockSpec((HALF, cols), lambda t: (0, 0))] * 4
        + [pl.BlockSpec((TILE, HALF), lambda t: (t, 0))] * 2
        + [pl.BlockSpec((TILE, HALF), lambda t: (t, 1))] * 2,
        out_specs=pl.BlockSpec((count, rows, cols), lambda t: (0, 0, 0)),
        out_shape=jax.ShapeDtypeStruct((count, rows, cols), I16),
        compiler_params=params(),
        cost_estimate=pl.CostEstimate(
            flops=12 * HALF * HALF * cols, transcendentals=0, bytes_accessed=1 << 23
        ),
        name="sine_rows",
    )(*drives, sy_hi, sy_lo, sy_hi, sy_lo)


def field_kernel(
    device,
    codes,
    even_hi,
    even_lo,
    odd_hi,
    odd_lo,
    x_near,
    x_far,
    yt,
    field,
    force,
    part_hi,
    part_lo,
    acc,
    *,
    steps,
    rows,
    count,
    sine,
):
    step = pl.program_id(0)
    flipped = device[0] >= count // 2

    @pl.when(step == 0)
    def _():
        if packable(rows):
            for pair in range(count // 2):
                near = decode(codes[2 * pair], steps)
                far = decode(codes[2 * pair + 1], steps)
                part = 2 * pair // (count // 2)
                here = pl.ds((pair % (count // 4)) * 128, 128)
                for half in range(2):
                    lanes = slice(half * 128, (half + 1) * 128)
                    for inner, value in enumerate(swap_halves((near[:, lanes], far[:, lanes]))):
                        lines = pl.ds((2 * half + inner) * rows, rows)
                        part_hi[part, lines, here], part_lo[part, lines, here] = split(value)
        else:
            for part in range(2):
                for block in range(PARTS):
                    here = pl.ds(block * TILE, TILE)
                    value = decode(codes[:, part * HALF + block * TILE :][:, :TILE], steps)
                    part_hi[part, :, here], part_lo[part, :, here] = split(value)

    even = dot3(part_hi[0], part_lo[0], even_hi[...], even_lo[...])
    odd = dot3(part_hi[1], part_lo[1], odd_hi[...], odd_lo[...])
    near = even + odd
    far = odd - even if sine else even - odd
    gathered = dot(near.astype(BF), x_near[...]) + dot(far.astype(BF), x_far[...])

    @pl.when(step == 0)
    def _():
        acc[...] = gathered

    @pl.when(step > 0)
    def _():
        acc[...] += gathered

    lane = 127 - lax.broadcasted_iota(jnp.int32, (8, 128), 1)
    sub = lax.broadcasted_iota(jnp.int32, (8, 128), 0)
    sub = jnp.where(flipped, 7 - sub, sub)
    for region in range(near.shape[0] // rows):
        for block in range(rows // 8):
            start = region * rows + 8 * block
            target = region * rows + jnp.where(flipped, rows - 8 - 8 * block, 8 * block)
            target = pl.multiple_of(target, 8)
            for tile in range(TILE // 128):
                piece = near[start : start + 8, tile * 128 : (tile + 1) * 128]
                piece = jnp.take_along_axis(piece, sub, axis=0)
                col = pl.multiple_of(step * TILE + tile * 128, 128)
                field[pl.ds(target, 8), pl.ds(col, 128)] = piece
                piece = far[start : start + 8, tile * 128 : (tile + 1) * 128]
                piece = jnp.take_along_axis(piece, sub, axis=0)
                piece = jnp.take_along_axis(piece, lane, axis=1)
                col = pl.multiple_of(M - 128 - step * TILE - tile * 128, 128)
                field[pl.ds(target, 8), pl.ds(col, 128)] = piece

    @pl.when(step == PARTS - 1)
    def _():
        force[...] = jnp.sum(yt[...].astype(F32) * acc[...], axis=0, keepdims=True)


def field_call(device, codes, even, odd, xt, yt, steps, rows, count, sine):
    lines, total = yt.shape
    zeros = (0,) * codes.ndim
    return pl.pallas_call(
        functools.partial(field_kernel, steps=steps, rows=rows, count=count, sine=sine),
        grid=(PARTS,),
        in_specs=[
            pl.BlockSpec(memory_space=pltpu.SMEM),
            pl.BlockSpec(codes.shape, lambda t: zeros),
        ]
        + [pl.BlockSpec((HALF, TILE), lambda t: (0, t))] * 2
        + [pl.BlockSpec((HALF, TILE), lambda t: (0, PARTS + t))] * 2
        + [
            pl.BlockSpec((TILE, total), lambda t: (t, 0)),
            pl.BlockSpec((TILE, total), lambda t: (PARTS + t, 0)),
            pl.BlockSpec((lines, total), lambda t: (0, 0)),
        ],
        out_specs=[
            pl.BlockSpec((lines, M), lambda t: (0, 0)),
            pl.BlockSpec((1, total), lambda t: (0, 0)),
        ],
        out_shape=[
            jax.ShapeDtypeStruct((lines, M), F32),
            jax.ShapeDtypeStruct((1, total), F32),
        ],
        scratch_shapes=[
            pltpu.VMEM((2, lines, HALF), BF),
            pltpu.VMEM((2, lines, HALF), BF),
            pltpu.VMEM((lines, total), F32),
        ],
        compiler_params=params(),
        cost_estimate=pl.CostEstimate(
            flops=2 * lines * M * (total + 3 * HALF), transcendentals=0, bytes_accessed=1 << 24
        ),
        name="field_x" if sine else "field_y",
    )(device, codes, even[0], even[1], odd[0], odd[1], xt, xt, yt)


def exchange(blocks):
    return lax.all_to_all(blocks, AXES, split_axis=0, concat_axis=0, tiled=True)


def work(cell_row, cell_col, cell_width, cell_height, cell_region, cell_offset):
    slab_count = lax.axis_size("slab")
    cell_count = lax.axis_size("cell")
    count = slab_count * cell_count
    device = lax.axis_index("slab") * cell_count + lax.axis_index("cell")
    rows = M // count
    own = cell_row.shape[0]
    lines = REGIONS * rows
    gain = math.sqrt(2.0 / M)
    fwd_steps = steps_of(2.1 * own * cell_count * WMAX * gain)
    back_steps = steps_of(gain**3 * own * count * WMAX * HMAX * 1.1 * M / math.pi * 8.5)

    ints = [cell_row, cell_col, cell_width, cell_height, cell_region]
    mine = jnp.concatenate(
        [jnp.stack(ints).astype(F32), cell_offset, jnp.zeros((1, own), F32)], axis=0
    )
    pieces = [mine]
    back_moves = []
    for turn in range(1, cell_count):
        pairs = [
            (slab * cell_count + c, slab * cell_count + (c + turn) % cell_count)
            for slab in range(slab_count)
            for c in range(cell_count)
        ]
        pieces.append(lax.ppermute(mine, AXES, pairs))
        back_moves.append([(b, a) for a, b in pairs])
    for c in range(cell_count):
        pairs = [
            (slab * cell_count + c, (slab + 1) * cell_count) for slab in range(slab_count - 1)
        ]
        pieces.append(lax.ppermute(mine, AXES, pairs))
        back_moves.append([(b, a) for a, b in pairs])
    tables = make_tables()
    cells = jnp.concatenate(pieces, axis=1)

    device = device.astype(jnp.int32).reshape(1)
    xt, yt, codes, sums = density_call(device, cells, tables, rows, count, fwd_steps)
    if not packable(rows):
        codes = jnp.transpose(codes.reshape(REGIONS, rows, count, rows), (2, 1, 0, 3))
        codes = codes.reshape(count, rows, lines)
    arrived = exchange(codes)
    drive = spectrum_call(device, arrived, tables, fwd_steps, back_steps)
    along_x = exchange(drive[0])
    sine_part = sine_call(drive[1:5], tables, count, rows, back_steps)
    along_y = exchange(sine_part)

    sums = jnp.concatenate([sums, drive[5]], axis=0)
    reach = 1
    while reach < count:
        sums = sums + lax.ppermute(sums, AXES, [(i, i ^ reach) for i in range(count)])
        reach *= 2
    sums = jnp.sum(sums.reshape(3, 8 * 128), axis=1)

    def lines_of(blocks):
        if packable(rows):
            return blocks
        shaped = blocks.reshape(count, rows, REGIONS, rows)
        return jnp.transpose(shaped, (2, 1, 0, 3)).reshape(lines, M)

    fwd, sy, ce, se = tables[0:2], tables[2:4], tables[4:6], tables[6:8]
    field_x, force_x = field_call(
        device, lines_of(along_x), se, sy, xt, yt, back_steps, rows, count, True
    )
    field_y, force_y = field_call(
        device, lines_of(along_y), ce, fwd, xt, yt, back_steps, rows, count, False
    )
    partial = jnp.concatenate([force_x, force_y], axis=0)
    cell_force = partial[:, :own]
    for index, pairs in enumerate(back_moves):
        piece = partial[:, (index + 1) * own : (index + 2) * own]
        cell_force = cell_force + lax.ppermute(piece, AXES, pairs)
    energy = sums[2] / (M * M)
    overflow = sums[0] / sums[1]
    shape = (REGIONS, rows, M)
    return (field_x.reshape(shape), field_y.reshape(shape), cell_force, energy, overflow)


def solution(mesh):
    return jax.shard_map(
        work,
        mesh=mesh,
        in_specs=(
            P(("slab", "cell")),
            P(("slab", "cell")),
            P(("slab", "cell")),
            P(("slab", "cell")),
            P(("slab", "cell")),
            P(None, ("slab", "cell")),
        ),
        out_specs=(
            P(None, ("slab", "cell"), None),
            P(None, ("slab", "cell"), None),
            P(None, ("slab", "cell")),
            P(),
            P(),
        ),
        check_vma=False,
    )
```

profile of v0, /device:TPU:0, one launch (start us, length us, event | category | flops | bytes accessed | tf_op | source)
XLA Modules:
  0.0 195.9 jit_solution(17281125483151747419)
XLA Ops:
  0.6 0.8 stack.23
  1.4 0.7 pad_maximum_fusion.1
  2.1 0.6 collective-permute-start
  2.7 4.4 %collective-permute-start.1 = (f32[8,512]{1,0:T(8,128)S(1)}, f32[8,512]{1,0:T(8,128)S(1)}, u32[]{:S(2)}, u32[]{:S(2)}) collective-permute-start(f32[8,512]{1,0:T(8,128)S(1)} %pad_maximum_fusion.1), channel_id=1, source_target_pairs={{0,2},{2,4},{4,6},{6,8},{8,10},{10,12},{12,14},{14,16},{16,18},{18... | collective-permute-start | bytes 49160 | tf_op jit(solution)/shard_map/ppermute | solution.py:606
  7.1 0.7 collective-permute-start.2
  7.8 10.8 %tables.1 = (bf16[1024,2048]{1,0:T(8,128)(2,1)}, bf16[1024,2048]{1,0:T(8,128)(2,1)}, bf16[1024,2048]{1,0:T(8,128)(2,1)}, bf16[1024,2048]{1,0:T(8,128)(2,1)}, bf1...) custom-call(f32[32,4,1024]{2,1,0:T(4,128)} %constant.21.clone.outer,, ...), custom_call_target="tpu_custom_call" | custom-call | flops 41943040 | bytes 25165824 | tf_op jit(solution)/shard_map/tables/pallas_call | solution.py:151
  18.5 0.0 collective-permute-done
  18.6 0.0 collective-permute-done.1
  18.6 0.0 collective-permute-done.2
  18.6 1.3 pad_maximum_fusion.cells
  19.9 18.3 %density.1 = (bf16[2048,2048]{1,0:T(8,128)(2,1)}, bf16[256,2048]{1,0:T(8,128)(2,1)}, s16[32,64,256]{2,1,0:T(8,128)(2,1)}, f32[16,128]{1,0:T(8,128)}) custom-call(s32[1]{0:T(128)} %bitcast.device, f32[8,2048]{1,0:T(8,128)} %pad_maximum_fusion.cells, bf16[1024,2048]{1,0:T(8,128)(2,1)} %get-tuple-element.27.fwd_hi.co_hi.ct_hi.odd_hi, ...), custom_call_target="tpu_custom_call" | custom-call | flops 5368709120 | bytes 16777216 | tf_op jit(solution)/shard_map/density/pallas_call | solution.py:272
  38.2 33.7 %all_to_all.15.codes = s16[32,64,256]{2,1,0:T(8,128)(2,1)} all-to-all(s16[32,64,256]{2,1,0:T(8,128)(2,1)} %get-tuple-element.29), channel_id=1, replica_groups=mesh['slab'=16,'cell'=2] {'slab','cell'}, dimensions={0} | all-to-all | bytes 2097152 | tf_op jit(solution)/shard_map/all_to_all | solution.py:573
  71.8 15.8 %spectrum.1 = (s16[32,64,256]{2,1,0:T(8,128)(2,1)}, bf16[1024,256]{1,0:T(8,128)(2,1)}, bf16[1024,256]{1,0:T(8,128)(2,1)}, bf16[1024,256]{1,0:T(8,128)(2,1)}, bf1...) custom-call(s32[1]{0:T(128)} %bitcast.device, s16[32,64,256]{2,1,0:T(8,128)(2,1)} %all_to_all.15.codes, ...), custom_call_target="tpu_custom_call" | custom-call | flops 6442450944 | bytes 16777216 | tf_op jit(solution)/shard_map/spectrum/pallas_call | solution.py:399
  87.7 8.3 %sine_rows.1 = s16[32,64,256]{2,1,0:T(8,128)(2,1)} custom-call(bf16[1024,256]{1,0:T(8,128)(2,1)} %get-tuple-element.40.dye_hi, bf16[1024,256]{1,0:T(8,128)(2,1)} %get-tuple-element.41.dye_lo, bf16[1024,256]{1,0:T(8,128)(2,1)} %get-tuple-element.42.dyo_hi, bf16[1024,256]{1,0:T(8,128)(2,1)} %get-tuple-element.43.dyo_lo, ...), custom_call_target="tpu_custom_call" | custom-call | flops 3221225472 | bytes 8388608 | tf_op jit(solution)/shard_map/sine_rows/pallas_call | solution.py:436
  96.0 0.0 copy-start.2
  96.0 0.0 copy-start.3
  96.0 29.9 %all_to_all.16.codes = s16[32,64,256]{2,1,0:T(8,128)(2,1)} all-to-all(s16[32,64,256]{2,1,0:T(8,128)(2,1)} %sine_rows.1), channel_id=1, replica_groups=mesh['slab'=16,'cell'=2] {'slab','cell'}, dimensions={0} | all-to-all | bytes 2097152 | tf_op jit(solution)/shard_map/all_to_all | solution.py:573
  126.0 3.8 %all-to-all-start.1 = ((s16[32,64,256]{2,1,0:T(8,128)(2,1)}), s16[32,64,256]{2,1,0:T(8,128)(2,1)S(1)}, u32[]{:S(2)}, u32[]{:S(2)}) async-start(s16[32,64,256]{2,1,0:T(8,128)(2,1)} %get-tuple-element.32), calls=%async_computation.1 | async-start | bytes 2097152 | tf_op jit(solution)/shard_map/all_to_all | solution.py:573
  129.8 0.0 copy-done.2
  129.8 0.0 copy-done.3
  129.8 0.1 collective-permute-start.6
  130.0 1.1 collective-permute-done.6
  131.1 1.6 collective-permute-start.7
  132.7 4.8 %collective-permute-done.7 = f32[24,128]{1,0:T(8,128)S(1)} collective-permute-done((f32[24,128]{1,0:T(8,128)S(1)}, f32[24,128]{1,0:T(8,128)S(1)}, u32[]{:S(2)}, u32[]{:S(2)}) %collective-permute-start.7) | collective-permute-done | bytes 12320 | tf_op jit(solution)/shard_map/ppermute | solution.py:625
  137.4 2.7 %collective-permute-start.8 = (f32[24,128]{1,0:T(8,128)S(1)}, f32[24,128]{1,0:T(8,128)S(1)}, u32[]{:S(2)}, u32[]{:S(2)}) collective-permute-start(f32[24,128]{1,0:T(8,128)S(1)} %add.32), channel_id=1, source_target_pairs={{0,4},{1,5},{2,6},{3,7},{4,0},{5,1},{6,2},{7,3},{8,12},{9,13},{10,... | collective-permute-start | bytes 36872 | tf_op jit(solution)/shard_map/ppermute | solution.py:625
  140.2 1.9 collective-permute-done.8
  142.1 0.3 collective-permute-start.9
  142.4 5.0 %collective-permute-done.9 = f32[24,128]{1,0:T(8,128)S(1)} collective-permute-done((f32[24,128]{1,0:T(8,128)S(1)}, f32[24,128]{1,0:T(8,128)S(1)}, u32[]{:S(2)}, u32[]{:S(2)}) %collective-permute-start.9) | collective-permute-done | bytes 12320 | tf_op jit(solution)/shard_map/ppermute | solution.py:625
  147.5 4.5 %collective-permute-start.10 = (f32[24,128]{1,0:T(8,128)S(1)}, f32[24,128]{1,0:T(8,128)S(1)}, u32[]{:S(2)}, u32[]{:S(2)}) collective-permute-start(f32[24,128]{1,0:T(8,128)S(1)} %add.34), channel_id=1, source_target_pairs={{0,16},{1,17},{2,18},{3,19},{4,20},{5,21},{6,22},{7,23},{8,24},{9,... | collective-permute-start | bytes 36872 | tf_op jit(solution)/shard_map/ppermute | solution.py:625
  152.0 4.4 %collective-permute-done.10 = f32[24,128]{1,0:T(8,128)S(1)} collective-permute-done((f32[24,128]{1,0:T(8,128)S(1)}, f32[24,128]{1,0:T(8,128)S(1)}, u32[]{:S(2)}, u32[]{:S(2)}) %collective-permute-start.10) | collective-permute-done | bytes 12320 | tf_op jit(solution)/shard_map/ppermute | solution.py:625
  156.3 0.1 add_reduce_fusion
  156.4 0.1 reduce_sum.14
  156.5 0.1 reduce_sum.18
  156.6 14.2 %field_y.1 = (f32[256,2048]{1,0:T(8,128)}, f32[1,2048]{1,0:T(1,128)}) custom-call(s32[1]{0:T(128)} %bitcast.device, s16[32,64,256]{2,1,0:T(8,128)(2,1)} %all_to_all.16.codes, bf16[1024,1024]{1,0:T(8,128)(2,1)} %get-tuple-element.30.ce_hi.even_hi, bf16[1024,1024]{1,0:T(8,128)(2,1)} %get-tuple-element.31.ce_lo.even_lo, ...), custom_call_target="tpu_custom_call" | custom-call | flops 5368709120 | bytes 16777216 | tf_op jit(solution)/shard_map/field_y/pallas_call | solution.py:537
  170.8 0.0 all-to-all-done.1.codes
  170.8 0.0 copy-start
  170.8 1.0 copy-done
  171.9 0.0 copy-start.1
  171.9 14.2 %field_x.1 = (f32[256,2048]{1,0:T(8,128)}, f32[1,2048]{1,0:T(1,128)}) custom-call(s32[1]{0:T(128)} %bitcast.device, s16[32,64,256]{2,1,0:T(8,128)(2,1)} %copy-done, bf16[1024,1024]{1,0:T(8,128)(2,1)} %get-tuple-element.33.even_hi, bf16[1024,1024]{1,0:T(8,128)(2,1)} %get-tuple-element.34.even_lo, bf16[1024,2048]{1,0:T(8,128)(2,1)} %get-tuple-element.35.odd_hi.se_hi.so_hi, ...), custom_call_target="tpu_custom_call" | custom-call | flops 5368709120 | bytes 16777216 | tf_op jit(solution)/shard_map/field_x/pallas_call | solution.py:537
  186.0 0.0 copy-done.1
  186.0 0.7 fusion.2
  186.7 0.1 collective-permute-start.3
  186.8 1.3 collective-permute-start.4
  188.1 0.7 collective-permute-start.5
  188.8 0.6 fusion.4
  191.3 0.0 collective-permute-done.3
  191.4 0.9 collective-permute-done.4
  192.3 0.0 collective-permute-done.5
  192.3 1.3 add_add_fusion
  (8 shorter events, 0.0 us)
Async XLA Ops:
  2.1 16.4 %collective-permute-start = (f32[8,512]{1,0:T(8,128)S(1)}, f32[8,512]{1,0:T(8,128)S(1)}, u32[]{:S(2)}, u32[]{:S(2)}) collective-permute-start(f32[8,512]{1,0:T(8,128)S(1)} %pad_maximum_fusion.1), channel_id=1, source_target_pairs={{0,1},{1,0},{2,3},{3,2},{4,5},{5,4},{6,7},{7,6},{8,9},{9,8},{10,11... | collective-permute-start | bytes 49160 | tf_op jit(solution)/shard_map/ppermute | solution.py:600
  2.7 15.9 %collective-permute-start.1 = (f32[8,512]{1,0:T(8,128)S(1)}, f32[8,512]{1,0:T(8,128)S(1)}, u32[]{:S(2)}, u32[]{:S(2)}) collective-permute-start(f32[8,512]{1,0:T(8,128)S(1)} %pad_maximum_fusion.1), channel_id=1, source_target_pairs={{0,2},{2,4},{4,6},{6,8},{8,10},{10,12},{12,14},{14,16},{16,18},{18... | collective-permute-start | bytes 49160 | tf_op jit(solution)/shard_map/ppermute | solution.py:606
  7.1 11.5 %collective-permute-start.2 = (f32[8,512]{1,0:T(8,128)S(1)}, f32[8,512]{1,0:T(8,128)S(1)}, u32[]{:S(2)}, u32[]{:S(2)}) collective-permute-start(f32[8,512]{1,0:T(8,128)S(1)} %pad_maximum_fusion.1), channel_id=1, source_target_pairs={{1,2},{3,4},{5,6},{7,8},{9,10},{11,12},{13,14},{15,16},{17,18},{19... | collective-permute-start | bytes 49160 | tf_op jit(solution)/shard_map/ppermute | solution.py:606
  96.0 33.8 %copy-start.2 = (f32[16,128]{1,0:T(8,128)S(1)}, f32[16,128]{1,0:T(8,128)}, u32[]{:S(2)}) copy-start(f32[16,128]{1,0:T(8,128)} %get-tuple-element.47) | copy-start | bytes 24580
  96.0 33.8 %copy-start.3 = (f32[8,128]{1,0:T(8,128)S(1)}, f32[8,128]{1,0:T(8,128)}, u32[]{:S(2)}) copy-start(f32[8,128]{1,0:T(8,128)} %get-tuple-element.48) | copy-start | bytes 12292
  126.0 44.9 %all-to-all-start.1 = ((s16[32,64,256]{2,1,0:T(8,128)(2,1)}), s16[32,64,256]{2,1,0:T(8,128)(2,1)S(1)}, u32[]{:S(2)}, u32[]{:S(2)}) async-start(s16[32,64,256]{2,1,0:T(8,128)(2,1)} %get-tuple-element.32), calls=%async_computation.1 | async-start | bytes 2097152 | tf_op jit(solution)/shard_map/all_to_all | solution.py:573
  129.8 1.2 collective-permute-start.6
  131.1 6.4 %collective-permute-start.7 = (f32[24,128]{1,0:T(8,128)S(1)}, f32[24,128]{1,0:T(8,128)S(1)}, u32[]{:S(2)}, u32[]{:S(2)}) collective-permute-start(f32[24,128]{1,0:T(8,128)S(1)} %add.31), channel_id=1, source_target_pairs={{0,2},{1,3},{2,0},{3,1},{4,6},{5,7},{6,4},{7,5},{8,10},{9,11},{10,... | collective-permute-start | bytes 36872 | tf_op jit(solution)/shard_map/ppermute | solution.py:625
  137.4 4.6 %collective-permute-start.8 = (f32[24,128]{1,0:T(8,128)S(1)}, f32[24,128]{1,0:T(8,128)S(1)}, u32[]{:S(2)}, u32[]{:S(2)}) collective-permute-start(f32[24,128]{1,0:T(8,128)S(1)} %add.32), channel_id=1, source_target_pairs={{0,4},{1,5},{2,6},{3,7},{4,0},{5,1},{6,2},{7,3},{8,12},{9,13},{10,... | collective-permute-start | bytes 36872 | tf_op jit(solution)/shard_map/ppermute | solution.py:625
  142.1 5.4 %collective-permute-start.9 = (f32[24,128]{1,0:T(8,128)S(1)}, f32[24,128]{1,0:T(8,128)S(1)}, u32[]{:S(2)}, u32[]{:S(2)}) collective-permute-start(f32[24,128]{1,0:T(8,128)S(1)} %add.33), channel_id=1, source_target_pairs={{0,8},{1,9},{2,10},{3,11},{4,12},{5,13},{6,14},{7,15},{8,0},{9,1},... | collective-permute-start | bytes 36872 | tf_op jit(solution)/shard_map/ppermute | solution.py:625
  147.5 8.9 %collective-permute-start.10 = (f32[24,128]{1,0:T(8,128)S(1)}, f32[24,128]{1,0:T(8,128)S(1)}, u32[]{:S(2)}, u32[]{:S(2)}) collective-permute-start(f32[24,128]{1,0:T(8,128)S(1)} %add.34), channel_id=1, source_target_pairs={{0,16},{1,17},{2,18},{3,19},{4,20},{5,21},{6,22},{7,23},{8,24},{9,... | collective-permute-start | bytes 36872 | tf_op jit(solution)/shard_map/ppermute | solution.py:625
  170.8 1.0 copy-start
  171.9 14.2 %copy-start.1 = (f32[1,2048]{1,0:T(1,128)S(1)}, f32[1,2048]{1,0:T(1,128)}, u32[]{:S(2)}) copy-start(f32[1,2048]{1,0:T(1,128)} %get-tuple-element.46) | copy-start | bytes 24580
  186.7 4.6 %collective-permute-start.3 = (f32[2,512]{1,0:T(2,128)S(1)}, f32[2,512]{1,0:T(2,128)S(1)}, u32[]{:S(2)}, u32[]{:S(2)}) collective-permute-start(f32[2,512]{1,0:T(2,128)S(1)} %get-tuple-element.49), channel_id=1, source_target_pairs={{1,0},{0,1},{3,2},{2,3},{5,4},{4,5},{7,6},{6,7},{9,8},{8,9},{11,10... | collective-permute-start | bytes 12296 | tf_op jit(solution)/shard_map/ppermute | solution.py:646
  186.8 5.5 %collective-permute-start.4 = (f32[2,512]{1,0:T(2,128)S(1)}, f32[2,512]{1,0:T(2,128)S(1)}, u32[]{:S(2)}, u32[]{:S(2)}) collective-permute-start(f32[2,512]{1,0:T(2,128)S(1)} %get-tuple-element.51), channel_id=1, source_target_pairs={{2,0},{4,2},{6,4},{8,6},{10,8},{12,10},{14,12},{16,14},{18,16},{20... | collective-permute-start | bytes 12296 | tf_op jit(solution)/shard_map/ppermute | solution.py:646
  188.1 4.2 %collective-permute-start.5 = (f32[2,512]{1,0:T(2,128)S(1)}, f32[2,512]{1,0:T(2,128)S(1)}, u32[]{:S(2)}, u32[]{:S(2)}) collective-permute-start(f32[2,512]{1,0:T(2,128)S(1)} %get-tuple-element.50), channel_id=1, source_target_pairs={{2,1},{4,3},{6,5},{8,7},{10,9},{12,11},{14,13},{16,15},{18,17},{20... | collective-permute-start | bytes 12296 | tf_op jit(solution)/shard_map/ppermute | solution.py:646
where the time goes:
time: 199 us; the launch traced here: 196 us
  Pallas kernels  81.5 us (41%)
  blocking collectives  63.6 us (32%)
  starting transfers between devices  20.8 us (10%)
  waiting for transfers between devices  18.1 us (9%)
  between operations  5.06 us (3%)
  other arithmetic  4.27 us (2%)
  local copies, waits for them, and re-layouts  2.49 us (1%)
    all_to_all x2, blocking collectives, exchange(): return lax.all_to_all(blocks, AXES, split_axis=0, concat_axis=0, tiled=True)  63.6 us
    pallas_call x2, Pallas kernels, field_call(): pl.pallas_call(functools.partial(field_kernel, steps=steps, rows=rows, co...  28.3 us
    pallas_call x1, Pallas kernels, density_call(): pl.pallas_call(functools.partial(density_kernel, steps=steps, rows=rows,...  18.3 us
    ppermute x5, waiting for transfers between devices, work(): lax.ppermute(sums, AXES, [(i, i ^ reach) for i in range(count)])  17.2 us
    pallas_call x1, Pallas kernels, spectrum_call(): pl.pallas_call(functools.partial(spectrum_kernel, fwd_steps=fwd_steps, ba...  15.8 us
    pallas_call x1, Pallas kernels, make_tables(): pl.pallas_call(table_kernel, grid=(HALF // (BAND * STRIP),), in_specs=[pl...  10.8 us
    ppermute x5, starting transfers between devices, work(): lax.ppermute(sums, AXES, [(i, i ^ reach) for i in range(count)])  9.33 us
    pallas_call x1, Pallas kernels, sine_call(): pl.pallas_call(functools.partial(sine_kernel, back_steps=back_steps), gri...  8.31 us
  transfers between devices with their start and end apart: 12, of which 6 were waited for; matrix products, arithmetic and copies ran while one was open for 0% of the time, Pallas kernels for 13%

commit v1 on v0

--- a/solution.py
+++ b/solution.py
@@ -475,7 +475,19 @@
 
     @pl.when(step == 0)
     def _():
-        if packable(rows):
+        if codes.ndim == 3 and codes.shape[2] % 512 == 0:
+            width = codes.shape[2] // REGIONS
+            sources = codes.shape[0]
+            for source in range(sources):
+                value = decode(codes[source], steps)
+                part = 2 * source // sources
+                here = pl.ds((source % (sources // 2)) * width, width)
+                for g in range(REGIONS):
+                    lines = pl.ds(g * rows, rows)
+                    high, low = split(value[:, g * width : (g + 1) * width])
+                    part_hi[part, lines, here] = high
+                    part_lo[part, lines, here] = low
+        elif packable(rows):
             for pair in range(count // 2):
                 near = decode(codes[2 * pair], steps)
                 far = decode(codes[2 * pair + 1], steps)
@@ -569,11 +581,341 @@
     )(device, codes, even[0], even[1], odd[0], odd[1], xt, xt, yt)
 
 
-def exchange(blocks):
-    return lax.all_to_all(blocks, AXES, split_axis=0, concat_axis=0, tiled=True)
-
-
-def work(cell_row, cell_col, cell_width, cell_height, cell_region, cell_offset):
+def profile(rel, low, extent):
+    high = jnp.minimum(rel + 1.0, low + extent)
+    return jnp.maximum(high - jnp.maximum(rel, low), 0.0)
+
+
+def local_kernel(device, cells, xt, yt, sums, dens, *, rows, count):
+    step = pl.program_id(0)
+    total = cells.shape[1]
+    chunk = 512
+
+    @pl.when(step == 0)
+    def _():
+        line = lax.broadcasted_iota(jnp.int32, (yt.shape[0], 1), 0)
+        inside = line & (rows - 1)
+        place = jnp.where(device[0] >= count // 2, rows - 1 - inside, inside) + device[0] * rows
+        place = place.astype(F32)
+        region = (line >> (rows.bit_length() - 1)).astype(F32)
+        for start in range(0, total, chunk):
+            here = pl.ds(start, chunk)
+            value = profile(place - cells[0:1, here], cells[6:7, here], cells[3:4, here])
+            yt[:, here] = jnp.where(region == cells[4:5, here], value, 0.0).astype(BF)
+        sums[...] = jnp.zeros((16, 128), F32)
+
+    place = (step % PARTS) * TILE + lax.broadcasted_iota(jnp.int32, (TILE, 1), 0)
+    place = jnp.where(step >= PARTS, M - 1 - place, place).astype(F32)
+    acc = None
+    for start in range(0, total, chunk):
+        here = pl.ds(start, chunk)
+        value = profile(place - cells[1:2, here], cells[5:6, here], cells[2:3, here]).astype(BF)
+        xt[:, here] = value
+        part = lax.dot_general(
+            yt[:, here], value, (((1,), (1,)), ((), ())), preferred_element_type=F32
+        )
+        acc = part if acc is None else acc + part
+    sums[0:8, :] += fold_rows(jnp.maximum(acc - 1.0, 0.0))
+    sums[8:16, :] += fold_rows(acc)
+
+
+def local_call(device, cells, rows, count):
+    total = cells.shape[1]
+    lines = REGIONS * rows
+    whole = lambda t: (0, 0)
+    return pl.pallas_call(
+        functools.partial(local_kernel, rows=rows, count=count),
+        grid=(2 * PARTS,),
+        in_specs=[
+            pl.BlockSpec(memory_space=pltpu.SMEM),
+            pl.BlockSpec((8, total), whole),
+        ],
+        out_specs=[
+            pl.BlockSpec((TILE, total), lambda t: (t, 0)),
+            pl.BlockSpec((lines, total), whole),
+            pl.BlockSpec((16, 128), whole),
+        ],
+        out_shape=[
+            jax.ShapeDtypeStruct((M, total), BF),
+            jax.ShapeDtypeStruct((lines, total), BF),
+            jax.ShapeDtypeStruct((16, 128), F32),
+        ],
+        scratch_shapes=[pltpu.VMEM((8, 128), F32)],
+        compiler_params=params(),
+        cost_estimate=pl.CostEstimate(
+            flops=2 * lines * M * total, transcendentals=0, bytes_accessed=1 << 23
+        ),
+        name="local",
+    )(device, cells)
+
+
+SPAN = 256
+EXTRA = 16
+
+
+def spectral_kernel(
+    device,
+    cells,
+    far_table,
+    near_table,
+    ce_hi,
+    ce_lo,
+    co_hi,
+    co_lo,
+    ct_hi,
+    ct_lo,
+    out,
+    dye_hi,
+    dye_lo,
+    dyo_hi,
+    dyo_lo,
+    energy,
+    dens,
+    far_hi,
+    far_lo,
+    near_both,
+    even_hi,
+    even_lo,
+    odd_hi,
+    odd_lo,
+    dxe_hi,
+    dxe_lo,
+    dxo_hi,
+    dxo_lo,
+    *,
+    slab_count,
+    count,
+    back_steps,
+):
+    step = pl.program_id(0)
+    slab_rows = M // slab_count
+    group = count // 2
+    rows = M // count
+    width = M // group
+    window = slab_rows + EXTRA
+    upper = device[0] >= group
+    member = jnp.where(upper, device[0] - group, device[0])
+    sign = jnp.where(upper, -1.0, 1.0).astype(F32)
+
+    @pl.when(step == 0)
+    def _():
+        dens[...] = jnp.zeros(dens.shape, F32)
+        far_hi[...], far_lo[...] = split(far_table[...])
+        near_both[:, : SPAN // 2], near_both[:, SPAN // 2 :] = split(near_table[...])
+        energy[...] = jnp.zeros((8, 128), F32)
+
+    @pl.when(step < slab_count)
+    def _():
+        top = step >= slab_count // 2
+        line = lax.broadcasted_iota(jnp.int32, (window, 1), 0)
+        line = jnp.where(top, window - 1 - line, line) + step * slab_rows
+        line = line.astype(F32)
+        turn = M.bit_length() - 1
+        acc = None
+        for piece in range(cells.shape[0]):
+            first = cells[piece, 0:1, :].astype(jnp.int32)
+            second = cells[piece, 1:2, :].astype(jnp.int32)
+            low_x = cells[piece, 2:3, :]
+            low_y = cells[piece, 3:4, :]
+            row = (first & (M - 1)).astype(F32)
+            region = (first >> turn) & (REGIONS - 1)
+            height = ((first >> (turn + 2)) + 1).astype(F32)
+            col = second & (M - 1)
+            wide = second >> turn
+            width_x = (wide + 1).astype(F32)
+            value_y = profile(line - row, low_y, height)
+            stacked = jnp.concatenate(
+                [jnp.where(region == g, value_y, 0.0).astype(BF) for g in range(REGIONS)], axis=0
+            )
+            head = profile(jnp.zeros_like(low_x), low_x, width_x)
+            tail = profile(width_x, low_x, width_x)
+            base = (col & 7) * 16
+            slot = lax.broadcasted_iota(jnp.int32, (SPAN // 2, 1), 0)
+            feature = jnp.where(slot == base + wide, 1.0, jnp.where(slot == base + 8 + wide, tail, 0.0))
+            feature = jnp.where(slot == base, head, feature).astype(BF)
+            spot = lax.broadcasted_iota(jnp.int32, (SPAN, 1), 0)
+            chosen = jnp.where(spot == (col >> 3), 1.0, 0.0).astype(BF)
+            near = dot(near_both[...], jnp.concatenate([feature, feature], axis=0))
+            far = dot(far_hi[...], chosen) + dot(far_lo[...], chosen)
+            value = near[:width] * far[:width] - near[width:] * far[width:]
+            value = jnp.concatenate(split(value), axis=0)
+            part = lax.dot_general(
+                stacked, value, (((1,), (1,)), ((), ())), preferred_element_type=F32
+            )
+            acc = part if acc is None else acc + part
+        half = jnp.where(top, 1, 0)
+        start = jnp.where(top, slab_count - 1 - step, step) * slab_rows
+        here = pl.ds(pl.multiple_of(start, 8), window)
+        for g in range(REGIONS):
+            lines = slice(g * window, (g + 1) * window)
+            lanes = pl.ds(g * width, width)
+            dens[half, here, lanes] += acc[lines, :width] + acc[lines, width:]
+
+    @pl.when(step == slab_count)
+    def _():
+        sub = 7 - lax.broadcasted_iota(jnp.int32, (8, 128), 0)
+        for tile in range(dens.shape[2] // 128):
+            lanes = pl.ds(tile * 128, 128)
+            spill = jnp.take_along_axis(dens[0, HALF : HALF + 8, lanes], sub, axis=0)
+            dens[1, HALF + EXTRA - 8 : HALF + EXTRA, lanes] += spill
+        for block in range(HALF // 128):
+            here = pl.ds(block * 128, 128)
+            near = dens[0, here, :]
+            mirrored = dens[1, pl.ds(block * 128 + EXTRA, 128), :]
+            even_hi[here, :], even_lo[here, :] = split(near + mirrored)
+            odd_hi[here, :], odd_lo[here, :] = split(near - mirrored)
+
+    @pl.when((step >= slab_count) & (step < slab_count + PARTS))
+    def _():
+        turn = step - slab_count
+        unit = math.pi / M
+        lane = lax.broadcasted_iota(jnp.int32, (1, REGIONS * width), 1) & (width - 1)
+        odd = jnp.where(member >= group // 2, 1, 0)
+        q = (2 * (width * (member - odd * (group // 2)) + lane) + odd).astype(F32)
+        first = lax.broadcasted_iota(jnp.int32, (TILE, 1), 0) + turn * TILE
+        here = pl.ds(pl.multiple_of(turn * TILE, TILE), TILE)
+
+        def solve(spectrum, p):
+            squared = p * p + q * q
+            inverse = jnp.where(squared == 0.0, 0.0, 1.0 / jnp.where(squared == 0.0, 1.0, squared))
+            scaled = spectrum * inverse
+            return scaled * (q * (1.0 / unit)), scaled * (p * (1.0 / unit)), spectrum * scaled
+
+        spec = dot3(ce_hi[...], ce_lo[...], even_hi[...], even_lo[...])
+        drive_x, drive_y, power = solve(spec, (2 * first).astype(F32))
+        dxe_hi[here, :], dxe_lo[here, :] = split(drive_x)
+        dye_hi[...], dye_lo[...] = split(drive_y * sign)
+        spec = dot3(co_hi[...], co_lo[...], odd_hi[...], odd_lo[...])
+        drive_x, drive_y, more = solve(spec, (2 * first + 1).astype(F32))
+        dxo_hi[here, :], dxo_lo[here, :] = split(drive_x * sign)
+        dyo_hi[...], dyo_lo[...] = split(drive_y)
+        energy[...] += fold_rows(power + more) * (1.0 / (unit * unit))
+
+    @pl.when(step >= slab_count + PARTS)
+    def _():
+        value = dot3(ct_hi[...], ct_lo[...], dxe_hi[...], dxe_lo[...])
+        value = value + dot3(co_hi[...], co_lo[...], dxo_hi[...], dxo_lo[...])
+        send_rows(out, (step - slab_count - PARTS) * (TILE // rows), value, upper, back_steps)
+
+
+def send_rows(out, first, value, upper, steps):
+    count, rows = out.shape[0], out.shape[1]
+    code = encode(value, steps)
+    for inner in range(TILE // rows):
+        target = first + inner
+        target = jnp.where(upper, count - 1 - target, target)
+        out[target] = code[inner * rows : (inner + 1) * rows]
+
+
+def spectral_call(device, cells, far_table, near_table, tables, slab_count, back_steps):
+    fwd_hi, fwd_lo, _, _, ce_hi, ce_lo, _, _ = tables
+    count = cells.shape[0]
+    group = count // 2
+    rows = M // count
+    width = M // group
+    cols = REGIONS * width
+    share = count // slab_count
+    phase = lambda t: jnp.clip(t - slab_count, 0, PARTS - 1)
+    last = lambda t: jnp.clip(t - slab_count - PARTS, 0, PARTS - 1)
+    both = lambda t: jnp.where(t < slab_count, 0, (t - slab_count) % PARTS)
+    drive = jax.ShapeDtypeStruct((HALF, cols), BF)
+    return pl.pallas_call(
+        functools.partial(
+            spectral_kernel, slab_count=slab_count, count=count, back_steps=back_steps
+        ),
+        grid=(slab_count + 2 * PARTS,),
+        in_specs=[
+            pl.BlockSpec(memory_space=pltpu.SMEM),
+            pl.BlockSpec(
+                (share,) + cells.shape[1:], lambda t: (jnp.minimum(t, slab_count - 1), 0, 0)
+            ),
+            pl.BlockSpec(far_table.shape, lambda t: (0, 0)),
+            pl.BlockSpec(near_table.shape, lambda t: (0, 0)),
+        ]
+        + [pl.BlockSpec((TILE, HALF), lambda t: (phase(t), 0))] * 2
+        + [pl.BlockSpec((TILE, HALF), lambda t: (both(t), 1))] * 2
+        + [pl.BlockSpec((TILE, HALF), lambda t: (last(t), 0))] * 2,
+        out_specs=[pl.BlockSpec((group, rows, cols), lambda t: (0, 0, 0))]
+        + [pl.BlockSpec((TILE, cols), lambda t: (phase(t), 0))] * 4
+        + [pl.BlockSpec((8, 128), lambda t: (0, 0))],
+        out_shape=[jax.ShapeDtypeStruct((group, rows, cols), I16)]
+        + [drive] * 4
+        + [jax.ShapeDtypeStruct((8, 128), F32)],
+        scratch_shapes=[
+            pltpu.VMEM((2, HALF + EXTRA, cols), F32),
+            pltpu.VMEM((2 * width, SPAN), BF),
+            pltpu.VMEM((2 * width, SPAN), BF),
+            pltpu.VMEM((2 * width, SPAN), BF),
+        ]
+        + [pltpu.VMEM((HALF, cols), BF)] * 8,
+        compiler_params=params(),
+        cost_estimate=pl.CostEstimate(
+            flops=30 * HALF * HALF * cols, transcendentals=0, bytes_accessed=1 << 24
+        ),
+        name="spectral",
+    )(device, cells, far_table, near_table, ce_hi, ce_lo, fwd_hi, fwd_lo, fwd_hi, fwd_lo)
+
+
+def sine_half_kernel(
+    device, dye_hi, dye_lo, dyo_hi, dyo_lo, se_hi, se_lo, so_hi, so_lo, out, *, back_steps
+):
+    value = dot3(se_hi[...], se_lo[...], dye_hi[...], dye_lo[...])
+    value = value + dot3(so_hi[...], so_lo[...], dyo_hi[...], dyo_lo[...])
+    first = pl.program_id(0) * (TILE // out.shape[1])
+    send_rows(out, first, value, device[0] >= out.shape[0], back_steps)
+
+
+def sine_half_call(device, drives, tables, group, rows, back_steps):
+    sy_hi, sy_lo = tables[2], tables[3]
+    cols = drives[0].shape[1]
+    return pl.pallas_call(
+        functools.partial(sine_half_kernel, back_steps=back_steps),
+        grid=(PARTS,),
+        in_specs=[pl.BlockSpec(memory_space=pltpu.SMEM)]
+        + [pl.BlockSpec((HALF, cols), lambda t: (0, 0))] * 4
+        + [pl.BlockSpec((TILE, HALF), lambda t: (t, 0))] * 2
+        + [pl.BlockSpec((TILE, HALF), lambda t: (t, 1))] * 2,
+        out_specs=pl.BlockSpec((group, rows, cols), lambda t: (0, 0, 0)),
+        out_shape=jax.ShapeDtypeStruct((group, rows, cols), I16),
+        compiler_params=params(),
+        cost_estimate=pl.CostEstimate(
+            flops=12 * HALF * HALF * cols, transcendentals=0, bytes_accessed=1 << 23
+        ),
+        name="sine_half",
+    )(device, *drives, sy_hi, sy_lo, sy_hi, sy_lo)
+
+
+def cell_tables(q):
+    odd = 2 * np.arange(16) + 1
+    moment = np.concatenate([16 * np.arange(SPAN), odd])
+    phase = (q[:, None] * jnp.asarray(moment, jnp.int32)[None, :]) % (4 * M)
+    angle = phase.astype(F32) * (math.pi / (2.0 * M))
+    both = jnp.concatenate([jnp.cos(angle), jnp.sin(angle)], axis=0)
+    weight = jnp.where(q == 0, math.sqrt(1.0 / M), math.sqrt(2.0 / M)).astype(F32)
+    far = both[:, :SPAN] * jnp.concatenate([weight, weight])[:, None]
+    chosen = np.zeros((16, 8, 16), np.float32)
+    for start in range(8):
+        chosen[start, start, 0] = 1.0
+        for wide in range(1, 9):
+            if wide > 1:
+                chosen[start + 1 : start + wide, start, wide - 1] = 1.0
+            chosen[start + wide, start, 7 + wide] = 1.0
+    near = jnp.dot(
+        both[:, SPAN:],
+        jnp.asarray(chosen.reshape(16, SPAN // 2)),
+        precision=lax.Precision.HIGHEST,
+        preferred_element_type=F32,
+    )
+    return far, near
+
+
+def exchange(blocks, groups=None):
+    return lax.all_to_all(
+        blocks, AXES, split_axis=0, concat_axis=0, tiled=True, axis_index_groups=groups
+    )
+
+
+def full_work(cell_row, cell_col, cell_width, cell_height, cell_region, cell_offset):
     slab_count = lax.axis_size("slab")
     cell_count = lax.axis_size("cell")
     count = slab_count * cell_count
@@ -650,6 +992,98 @@
     return (field_x.reshape(shape), field_y.reshape(shape), cell_force, energy, overflow)
 
 
+def half_work(cell_row, cell_col, cell_width, cell_height, cell_region, cell_offset):
+    slab_count = lax.axis_size("slab")
+    cell_count = lax.axis_size("cell")
+    count = slab_count * cell_count
+    group = count // 2
+    slab = lax.axis_index("slab")
+    member = lax.axis_index("cell")
+    device = slab * cell_count + member
+    rows = M // count
+    width = M // group
+    own = cell_row.shape[0]
+    gain = math.sqrt(2.0 / M)
+    back_steps = steps_of(gain**3 * own * count * WMAX * HMAX * 1.1 * M / math.pi * 8.5)
+    groups = [list(range(group)), list(range(group, count))]
+
+    first = cell_row + M * (cell_region + REGIONS * (cell_height - 1))
+    second = cell_col + M * (cell_width - 1)
+    mine = jnp.concatenate([jnp.stack([first, second]).astype(F32), cell_offset], axis=0)
+    everyone = exchange(jnp.broadcast_to(mine[None], (count,) + mine.shape))
+    tables = make_tables()
+    within = device % group
+    odd = within // (group // 2)
+    q = 2 * (width * (within - odd * (group // 2)) + lax.iota(jnp.int32, width)) + odd
+    far_table, near_table = cell_tables(q)
+    scalar = device.astype(jnp.int32).reshape(1)
+
+    drive = spectral_call(scalar, everyone, far_table, near_table, tables, slab_count, back_steps)
+    along_x = exchange(drive[0], groups)
+    sine_part = sine_half_call(scalar, drive[1:5], tables, group, rows, back_steps)
+    along_y = exchange(sine_part, groups)
+
+    begin = jnp.maximum(slab - 1, 0) * cell_count
+    below = lax.dynamic_slice_in_dim(everyone, begin, cell_count)
+    level = lax.dynamic_slice_in_dim(everyone, slab * cell_count, cell_count)
+    near_cells = jnp.concatenate([level, below], axis=0)
+    low = near_cells[:, 0].astype(jnp.int32)
+    wide = near_cells[:, 1].astype(jnp.int32)
+    turn = M.bit_length() - 1
+    block = lax.iota(jnp.int32, 2 * cell_count)[:, None]
+    used = (block < cell_count) | ((member == 0) & (slab > 0))
+    used = used.astype(F32)
+    region = (low >> turn) & (REGIONS - 1)
+    region = jnp.where(used > 0.0, region, REGIONS)
+    fields = [
+        (low & (M - 1)).astype(F32),
+        (wide & (M - 1)).astype(F32),
+        ((wide >> turn) + 1).astype(F32),
+        ((low >> (turn + 2)) + 1).astype(F32),
+        region.astype(F32),
+        near_cells[:, 2],
+        near_cells[:, 3],
+        near_cells[:, 3],
+    ]
+    cells = jnp.stack(fields).reshape(8, 2 * cell_count * own)
+    xt, yt, sums = local_call(scalar, cells, rows, count)
+
+    sums = jnp.concatenate([sums, drive[5]], axis=0)
+    reach = 1
+    while reach < count:
+        sums = sums + lax.ppermute(sums, AXES, [(i, i ^ reach) for i in range(count)])
+        reach *= 2
+    sums = jnp.sum(sums.reshape(3, 8 * 128), axis=1)
+
+    fwd, sy, ce, se = tables[0:2], tables[2:4], tables[4:6], tables[6:8]
+    field_x, force_x = field_call(scalar, along_x, se, sy, xt, yt, back_steps, rows, count, True)
+    field_y, force_y = field_call(scalar, along_y, ce, fwd, xt, yt, back_steps, rows, count, False)
+    partial = jnp.concatenate([force_x, force_y], axis=0).reshape(2, 2 * cell_count, own)
+    cell_force = lax.dynamic_index_in_dim(partial, member, 1, keepdims=False)
+    for turn in range(1, cell_count):
+        piece = lax.dynamic_index_in_dim(partial, (member + turn) % cell_count, 1, keepdims=False)
+        pairs = [
+            (s * cell_count + c, s * cell_count + (c + turn) % cell_count)
+            for s in range(slab_count)
+            for c in range(cell_count)
+        ]
+        cell_force = cell_force + lax.ppermute(piece, AXES, pairs)
+    for c in range(cell_count):
+        pairs = [(s * cell_count, (s - 1) * cell_count + c) for s in range(1, slab_count)]
+        cell_force = cell_force + lax.ppermute(partial[:, cell_count + c], AXES, pairs)
+    energy = sums[2] / (2 * M * M)
+    overflow = sums[0] / sums[1]
+    shape = (REGIONS, rows, M)
+    return (field_x.reshape(shape), field_y.reshape(shape), cell_force, energy, overflow)
+
+
+def work(*args):
+    count = lax.axis_size("slab") * lax.axis_size("cell")
+    if packable(M // count):
+        return half_work(*args)
+    return full_work(*args)
+
+
 def solution(mesh):
     return jax.shard_map(
         work,

time: 199 us -> 176 us (0.88)
  blocking collectives: 63.6 us -> 21.2 us
  Pallas kernels: 81.5 us -> 103 us
  waiting for transfers between devices: 18.1 us -> 10.6 us
  local copies, waits for them, and re-layouts: 2.49 us -> 5.43 us
    all_to_all x2 -> x1, blocking collectives: 63.6 us -> 21.2 us  [exchange(): lax.all_to_all(blocks, AXES, split_axis=0, concat_axis=0, tiled=True, axi...]
    pallas_call x3, Pallas kernels: 42.4 us -> 64.3 us  [the longest x1 43.8 us: spectral_call(): pl.pallas_call(functools.partial(spectral_kernel, slab_count=slab_count,...]
    ppermute x11 -> x8, starting transfers between devices: 17 us -> 9.24 us  [the longest x5 7.21 us: half_work(): lax.ppermute(sums, AXES, [(i, i ^ reach) for i in range(count)])]
    ppermute x11 -> x8, waiting for transfers between devices: 18.1 us -> 10.6 us  [the longest x5 9.65 us: half_work(): lax.ppermute(sums, AXES, [(i, i ^ reach) for i in range(count)])]
    all_to_all x1 -> x2, starting transfers between devices: 3.8 us -> 11.2 us  [exchange(): lax.all_to_all(blocks, AXES, split_axis=0, concat_axis=0, tiled=True, axi...]
  transfers between devices with their start and end apart: 12 -> 10, of which waited for: 6 -> 6; matrix products, arithmetic and copies ran while one was open for 0% -> 4% of each run, Pallas kernels for 13% -> 19%
where the time goes in v1:
time: 176 us; the launch traced here: 173 us
  Pallas kernels  103 us (59%)
  blocking collectives  21.2 us (12%)
  starting transfers between devices  20.4 us (12%)
  waiting for transfers between devices  10.6 us (6%)
  other arithmetic  6.17 us (4%)
  local copies, waits for them, and re-layouts  5.43 us (3%)
  between operations  5.11 us (3%)
    pallas_call x1, Pallas kernels, spectral_call(): pl.pallas_call(functools.partial(spectral_kernel, slab_count=slab_count,...  43.8 us
    pallas_call x2, Pallas kernels, field_call(): pl.pallas_call(functools.partial(field_kernel, steps=steps, rows=rows, co...  28.1 us
    all_to_all x1, blocking collectives, exchange(): lax.all_to_all(blocks, AXES, split_axis=0, concat_axis=0, tiled=True, axi...  21.2 us
    pallas_call x1, Pallas kernels, sine_half_call(): pl.pallas_call(functools.partial(sine_half_kernel, back_steps=back_steps)...  11.7 us
    all_to_all x2, starting transfers between devices, exchange(): lax.all_to_all(blocks, AXES, split_axis=0, concat_axis=0, tiled=True, axi...  11.2 us
    pallas_call x1, Pallas kernels, make_tables(): pl.pallas_call(table_kernel, grid=(HALF // (BAND * STRIP),), in_specs=[pl...  10.8 us
    ppermute x5, waiting for transfers between devices, half_work(): lax.ppermute(sums, AXES, [(i, i ^ reach) for i in range(count)])  9.65 us
    pallas_call x1, Pallas kernels, local_call(): pl.pallas_call(functools.partial(local_kernel, rows=rows, count=count), g...  8.76 us
  transfers between devices with their start and end apart: 10, of which 6 were waited for; matrix products, arithmetic and copies ran while one was open for 4% of the time, Pallas kernels for 19%

profile of v1, /device:TPU:0, one launch (start us, length us, event | category | flops | bytes accessed | tf_op | source)
XLA Modules:
  0.0 173.0 jit_solution(3808032725191681908)
XLA Ops:
  0.6 0.0 copy-start.2
  0.6 0.7 multiply_add_fusion
  1.4 0.7 multiply_add_fusion.1
  2.1 0.7 pad_maximum_fusion.4
  2.8 0.7 broadcast_in_dim.30
  3.5 7.3 %all-to-all-start = ((f32[32,4,512]{2,1,0:T(4,128)}), f32[32,4,512]{2,1,0:T(4,128)S(1)}, u32[]{:S(2)}, u32[]{:S(2)}) async-start(f32[32,4,512]{2,1,0:T(4,128)} %broadcast_in_dim.30), calls=%async_computation | async-start | bytes 524288 | tf_op jit(solution)/shard_map/all_to_all | solution.py:913
  10.9 1.5 fusion.7
  12.5 10.8 %tables.1 = (bf16[1024,2048]{1,0:T(8,128)(2,1)}, bf16[1024,2048]{1,0:T(8,128)(2,1)}, bf16[1024,2048]{1,0:T(8,128)(2,1)}, bf16[1024,2048]{1,0:T(8,128)(2,1)}, bf1...) custom-call(f32[32,4,1024]{2,1,0:T(4,128)} %constant.113.clone.outer, ...), custom_call_target="tpu_custom_call" | custom-call | flops 41943040 | bytes 25165824 | tf_op jit(solution)/shard_map/tables/pallas_call | solution.py:151
  23.2 0.0 copy-done.2
  23.3 0.9 fusion.5.near_table
  24.2 0.8 fusion.1.far_table
  25.0 0.0 all-to-all-done.cells
  25.0 0.0 copy-start.1
  25.0 0.7 copy-done.1
  25.7 43.8 %spectral.1 = (s16[16,64,512]{2,1,0:T(8,128)(2,1)}, bf16[1024,512]{1,0:T(8,128)(2,1)}, bf16[1024,512]{1,0:T(8,128)(2,1)}, bf16[1024,512]{1,0:T(8,128)(2,1)}, bf1...) custom-call(s32[1]{0:T(128)} %bitcast.device, f32[32,4,512]{2,1,0:T(4,128)} %copy-done.1, f32[256,256]{1,0:T(8,128)} %fusion.1.far_table, ...), custom_call_target="tpu_custom_call" | custom-call | flops 16106127360 | bytes 16777216 | tf_op jit(solution)/shard_map/spectral/pallas_call | solution.py:822
  69.5 11.7 %sine_half.1 = s16[16,64,512]{2,1,0:T(8,128)(2,1)} custom-call(s32[1]{0:T(128)} %bitcast.device, bf16[1024,512]{1,0:T(8,128)(2,1)} %get-tuple-element.38.dye_hi, bf16[1024,512]{1,0:T(8,128)(2,1)} %get-tuple-element.39.dye_lo, bf16[1024,512]{1,0:T(8,128)(2,1)} %get-tuple-element.40.dyo_hi, bf16[1024,512]{1,0:T(8,128)(2,1)} %get-tuple-element.41.dyo_lo, ...), custom_call_target="tpu_custom_call" | custom-call | flops 6442450944 | bytes 8388608 | tf_op jit(solution)/shard_map/sine_half/pallas_call | solution.py:871
  81.2 21.2 %all_to_all.15.codes = s16[16,64,512]{2,1,0:T(8,128)(2,1)} all-to-all(s16[16,64,512]{2,1,0:T(8,128)(2,1)} %sine_half.1), channel_id=1, replica_groups={{0,1,2,3,4,5,6,7,8,9,10,11,12,13,14,15},{16,17,18,19,20,21,22,23,24,25,..., dimensions={0} | all-to-all | bytes 2097152 | tf_op jit(solution)/shard_map/all_to_all | solution.py:913
  102.4 3.8 %all-to-all-start.1 = ((s16[16,64,512]{2,1,0:T(8,128)(2,1)}), s16[16,64,512]{2,1,0:T(8,128)(2,1)S(1)}, u32[]{:S(2)}, u32[]{:S(2)}) async-start(s16[16,64,512]{2,1,0:T(8,128)(2,1)} %get-tuple-element.30), calls=%async_computation.1 | async-start | bytes 2097152 | tf_op jit(solution)/shard_map/all_to_all | solution.py:913
  106.2 0.8 constant_dynamic-slice_fusion.3
  107.1 0.1 add_convert_fusion.1
  107.2 0.7 stack.26.cells
  107.9 0.0 copy-start.4
  107.9 8.8 %local.1 = (bf16[2048,2048]{1,0:T(8,128)(2,1)}, bf16[256,2048]{1,0:T(8,128)(2,1)}, f32[16,128]{1,0:T(8,128)}) custom-call(s32[1]{0:T(128)} %bitcast.device, f32[8,2048]{1,0:T(8,128)} %stack.26.cells), custom_call_target="tpu_custom_call" | custom-call | flops 2147483648 | bytes 8388608 | tf_op jit(solution)/shard_map/local/pallas_call | solution.py:626
  116.7 0.7 constant_dynamic-update-slice_fusion.1
  117.4 0.0 copy-done.4
  117.4 0.1 collective-permute-start.3
  117.5 1.1 collective-permute-done.3
  118.5 1.6 collective-permute-start.4
  120.1 2.1 %collective-permute-done.4 = f32[24,128]{1,0:T(8,128)S(1)} collective-permute-done((f32[24,128]{1,0:T(8,128)S(1)}, f32[24,128]{1,0:T(8,128)S(1)}, u32[]{:S(2)}, u32[]{:S(2)}) %collective-permute-start.4) | collective-permute-done | bytes 12320 | tf_op jit(solution)/shard_map/ppermute | solution.py:1054
  122.2 1.6 collective-permute-start.5
  123.8 2.1 %collective-permute-done.5 = f32[24,128]{1,0:T(8,128)S(1)} collective-permute-done((f32[24,128]{1,0:T(8,128)S(1)}, f32[24,128]{1,0:T(8,128)S(1)}, u32[]{:S(2)}, u32[]{:S(2)}) %collective-permute-start.5) | collective-permute-done | bytes 12320 | tf_op jit(solution)/shard_map/ppermute | solution.py:1054
  125.9 1.6 collective-permute-start.6
  127.5 2.1 %collective-permute-done.6 = f32[24,128]{1,0:T(8,128)S(1)} collective-permute-done((f32[24,128]{1,0:T(8,128)S(1)}, f32[24,128]{1,0:T(8,128)S(1)}, u32[]{:S(2)}, u32[]{:S(2)}) %collective-permute-start.6) | collective-permute-done | bytes 12320 | tf_op jit(solution)/shard_map/ppermute | solution.py:1054
  129.6 2.4 %collective-permute-start.7 = (f32[24,128]{1,0:T(8,128)S(1)}, f32[24,128]{1,0:T(8,128)S(1)}, u32[]{:S(2)}, u32[]{:S(2)}) collective-permute-start(f32[24,128]{1,0:T(8,128)S(1)} %add.137), channel_id=1, source_target_pairs={{0,16},{1,17},{2,18},{3,19},{4,20},{5,21},{6,22},{7,23},{8,24},{9,... | collective-permute-start | bytes 36872 | tf_op jit(solution)/shard_map/ppermute | solution.py:1054
  132.1 2.2 %collective-permute-done.7 = f32[24,128]{1,0:T(8,128)S(1)} collective-permute-done((f32[24,128]{1,0:T(8,128)S(1)}, f32[24,128]{1,0:T(8,128)S(1)}, u32[]{:S(2)}, u32[]{:S(2)}) %collective-permute-start.7) | collective-permute-done | bytes 12320 | tf_op jit(solution)/shard_map/ppermute | solution.py:1054
  134.2 0.1 add_reduce_fusion
  134.4 0.1 reduce_sum.14
  134.4 0.1 reduce_sum.18
  134.6 14.1 %field_y.1 = (f32[256,2048]{1,0:T(8,128)}, f32[1,2048]{1,0:T(1,128)}) custom-call(s32[1]{0:T(128)} %bitcast.device, s16[16,64,512]{2,1,0:T(8,128)(2,1)} %all_to_all.15.codes, bf16[1024,1024]{1,0:T(8,128)(2,1)} %get-tuple-element.26.ce_hi.even_hi, bf16[1024,1024]{1,0:T(8,128)(2,1)} %get-tuple-element.27.ce_lo.even_lo, ...), custom_call_target="tpu_custom_call" | custom-call | flops 5368709120 | bytes 16777216 | tf_op jit(solution)/shard_map/field_y/pallas_call | solution.py:549
  148.6 0.0 all-to-all-done.1.codes
  148.6 0.0 copy-start
  148.7 1.0 copy-done
  149.7 0.0 copy-start.3
  149.7 14.1 %field_x.1 = (f32[256,2048]{1,0:T(8,128)}, f32[1,2048]{1,0:T(1,128)}) custom-call(s32[1]{0:T(128)} %bitcast.device, s16[16,64,512]{2,1,0:T(8,128)(2,1)} %copy-done, bf16[1024,1024]{1,0:T(8,128)(2,1)} %get-tuple-element.31.even_hi, bf16[1024,1024]{1,0:T(8,128)(2,1)} %get-tuple-element.32.even_lo, bf16[1024,2048]{1,0:T(8,128)(2,1)} %get-tuple-element.33.odd_hi.se_hi.so_hi, ...), custom_call_target="tpu_custom_call" | custom-call | flops 5368709120 | bytes 16777216 | tf_op jit(solution)/shard_map/field_x/pallas_call | solution.py:549
  163.8 0.0 copy-done.3
  163.8 0.7 pad_maximum_fusion.2
  164.5 0.1 collective-permute-start
  164.6 1.3 collective-permute-start.1
  165.9 0.7 collective-permute-start.2
  166.6 0.6 fusion.19
  169.2 0.0 collective-permute-done
  169.2 0.9 collective-permute-done.1
  170.1 0.0 collective-permute-done.2
  170.1 0.6 fusion.14
  (15 shorter events, 0.1 us)
Async XLA Ops:
  0.6 22.6 %copy-start.2 = (f32[16,128]{1,0:T(8,128)S(1)}, f32[16,128]{1,0:T(8,128)}, u32[]{:S(2)}) copy-start(f32[16,128]{1,0:T(8,128)} %constant.116.clone) | copy-start | bytes 24580
  3.5 21.4 %all-to-all-start = ((f32[32,4,512]{2,1,0:T(4,128)}), f32[32,4,512]{2,1,0:T(4,128)S(1)}, u32[]{:S(2)}, u32[]{:S(2)}) async-start(f32[32,4,512]{2,1,0:T(4,128)} %broadcast_in_dim.30), calls=%async_computation | async-start | bytes 524288 | tf_op jit(solution)/shard_map/all_to_all | solution.py:913
  25.0 0.7 copy-start.1
  102.4 46.3 %all-to-all-start.1 = ((s16[16,64,512]{2,1,0:T(8,128)(2,1)}), s16[16,64,512]{2,1,0:T(8,128)(2,1)S(1)}, u32[]{:S(2)}, u32[]{:S(2)}) async-start(s16[16,64,512]{2,1,0:T(8,128)(2,1)} %get-tuple-element.30), calls=%async_computation.1 | async-start | bytes 2097152 | tf_op jit(solution)/shard_map/all_to_all | solution.py:913
  107.9 9.5 %copy-start.4 = (f32[8,128]{1,0:T(8,128)S(1)}, f32[8,128]{1,0:T(8,128)}, u32[]{:S(2)}) copy-start(f32[8,128]{1,0:T(8,128)} %get-tuple-element.46) | copy-start | bytes 12292
  117.4 1.2 collective-permute-start.3
  118.5 3.7 %collective-permute-start.4 = (f32[24,128]{1,0:T(8,128)S(1)}, f32[24,128]{1,0:T(8,128)S(1)}, u32[]{:S(2)}, u32[]{:S(2)}) collective-permute-start(f32[24,128]{1,0:T(8,128)S(1)} %add.134), channel_id=1, source_target_pairs={{0,2},{1,3},{2,0},{3,1},{4,6},{5,7},{6,4},{7,5},{8,10},{9,11},{10,... | collective-permute-start | bytes 36872 | tf_op jit(solution)/shard_map/ppermute | solution.py:1054
  122.2 3.7 %collective-permute-start.5 = (f32[24,128]{1,0:T(8,128)S(1)}, f32[24,128]{1,0:T(8,128)S(1)}, u32[]{:S(2)}, u32[]{:S(2)}) collective-permute-start(f32[24,128]{1,0:T(8,128)S(1)} %add.135), channel_id=1, source_target_pairs={{0,4},{1,5},{2,6},{3,7},{4,0},{5,1},{6,2},{7,3},{8,12},{9,13},{10,... | collective-permute-start | bytes 36872 | tf_op jit(solution)/shard_map/ppermute | solution.py:1054
  125.9 3.7 %collective-permute-start.6 = (f32[24,128]{1,0:T(8,128)S(1)}, f32[24,128]{1,0:T(8,128)S(1)}, u32[]{:S(2)}, u32[]{:S(2)}) collective-permute-start(f32[24,128]{1,0:T(8,128)S(1)} %add.136), channel_id=1, source_target_pairs={{0,8},{1,9},{2,10},{3,11},{4,12},{5,13},{6,14},{7,15},{8,0},{9,1},... | collective-permute-start | bytes 36872 | tf_op jit(solution)/shard_map/ppermute | solution.py:1054
  129.6 4.6 %collective-permute-start.7 = (f32[24,128]{1,0:T(8,128)S(1)}, f32[24,128]{1,0:T(8,128)S(1)}, u32[]{:S(2)}, u32[]{:S(2)}) collective-permute-start(f32[24,128]{1,0:T(8,128)S(1)} %add.137), channel_id=1, source_target_pairs={{0,16},{1,17},{2,18},{3,19},{4,20},{5,21},{6,22},{7,23},{8,24},{9,... | collective-permute-start | bytes 36872 | tf_op jit(solution)/shard_map/ppermute | solution.py:1054
  148.6 1.0 copy-start
  149.7 14.1 %copy-start.3 = (f32[1,2048]{1,0:T(1,128)S(1)}, f32[1,2048]{1,0:T(1,128)}, u32[]{:S(2)}) copy-start(f32[1,2048]{1,0:T(1,128)} %get-tuple-element.44) | copy-start | bytes 24580
  164.5 4.6 %collective-permute-start = (f32[2,512]{1,0:T(2,128)S(1)}, f32[2,512]{1,0:T(2,128)S(1)}, u32[]{:S(2)}, u32[]{:S(2)}) collective-permute-start(f32[2,512]{1,0:T(2,128)S(1)} %bitcast.41), channel_id=1, source_target_pairs={{0,1},{1,0},{2,3},{3,2},{4,5},{5,4},{6,7},{7,6},{8,9},{9,8},{10,11... | collective-permute-start | bytes 12296 | tf_op jit(solution)/shard_map/ppermute | solution.py:1070
  164.6 5.5 %collective-permute-start.1 = (f32[2,512]{1,0:T(2,128)S(1)}, f32[2,512]{1,0:T(2,128)S(1)}, u32[]{:S(2)}, u32[]{:S(2)}) collective-permute-start(f32[2,512]{1,0:T(2,128)S(1)} %get-tuple-element.61), channel_id=1, source_target_pairs={{2,0},{4,2},{6,4},{8,6},{10,8},{12,10},{14,12},{16,14},{18,16},{20... | collective-permute-start | bytes 12296 | tf_op jit(solution)/shard_map/ppermute | solution.py:1073
  165.9 4.2 %collective-permute-start.2 = (f32[2,512]{1,0:T(2,128)S(1)}, f32[2,512]{1,0:T(2,128)S(1)}, u32[]{:S(2)}, u32[]{:S(2)}) collective-permute-start(f32[2,512]{1,0:T(2,128)S(1)} %get-tuple-element.62), channel_id=1, source_target_pairs={{2,1},{4,3},{6,5},{8,7},{10,9},{12,11},{14,13},{16,15},{18,17},{20... | collective-permute-start | bytes 12296 | tf_op jit(solution)/shard_map/ppermute | solution.py:1073

commit v2 on v1

--- a/solution.py
+++ b/solution.py
@@ -117,7 +117,11 @@
     return outer.astype(np.float32), inner.astype(np.float32)
 
 
-def table_kernel(outer, inner, fwd_hi, fwd_lo, sy_hi, sy_lo, ce_hi, ce_lo, se_hi, se_lo):
+def table_kernel(device, outer, inner, fwd_hi, fwd_lo, sy_hi, sy_lo, ce_hi, ce_lo, se_hi, se_lo, look):
+    @pl.when(pl.program_id(0) == 0)
+    def _():
+        look[...] = cell_tables(device[0], look.shape[0] // 4)
+
     for group in range(BAND):
         here = pl.ds(group * STRIP, STRIP)
 
@@ -142,7 +146,7 @@
         sy_hi[here, :HALF], sy_lo[here, :HALF] = split(sin_t)
 
 
-def make_tables():
+def make_tables(first_q, width):
     outer, inner = base_tables()
     wide = jax.ShapeDtypeStruct((HALF, M), BF)
     square = jax.ShapeDtypeStruct((HALF, HALF), BF)
@@ -152,17 +156,22 @@
         table_kernel,
         grid=(HALF // (BAND * STRIP),),
         in_specs=[
+            pl.BlockSpec(memory_space=pltpu.SMEM),
             pl.BlockSpec((BAND, 4, HALF), lambda g: (g, 0, 0)),
             pl.BlockSpec((6, STRIP, HALF), lambda g: (0, 0, 0)),
         ],
-        out_specs=[wide_spec] * 4 + [square_spec] * 4,
-        out_shape=[wide] * 4 + [square] * 4,
+        out_specs=[wide_spec] * 4
+        + [square_spec] * 4
+        + [pl.BlockSpec((4 * width, 2 * LOOK), lambda g: (0, 0))],
+        out_shape=[wide] * 4
+        + [square] * 4
+        + [jax.ShapeDtypeStruct((4 * width, 2 * LOOK), F32)],
         compiler_params=params(),
         cost_estimate=pl.CostEstimate(
             flops=40 * HALF * HALF, transcendentals=0, bytes_accessed=24 * HALF * HALF
         ),
         name="tables",
-    )(jnp.asarray(outer), jnp.asarray(inner))
+    )(first_q, jnp.asarray(outer), jnp.asarray(inner))
 
 
 def fold_rows(value):
@@ -469,24 +478,20 @@
     rows,
     count,
     sine,
+    by_half,
 ):
     step = pl.program_id(0)
     flipped = device[0] >= count // 2
 
     @pl.when(step == 0)
     def _():
-        if codes.ndim == 3 and codes.shape[2] % 512 == 0:
-            width = codes.shape[2] // REGIONS
-            sources = codes.shape[0]
+        if by_half:
+            sources, width = codes.shape[0], codes.shape[2]
             for source in range(sources):
-                value = decode(codes[source], steps)
+                value = decode(codes[source, 0 : REGIONS * rows, :], steps)
                 part = 2 * source // sources
                 here = pl.ds((source % (sources // 2)) * width, width)
-                for g in range(REGIONS):
-                    lines = pl.ds(g * rows, rows)
-                    high, low = split(value[:, g * width : (g + 1) * width])
-                    part_hi[part, lines, here] = high
-                    part_lo[part, lines, here] = low
+                part_hi[part, :, here], part_lo[part, :, here] = split(value)
         elif packable(rows):
             for pair in range(count // 2):
                 near = decode(codes[2 * pair], steps)
@@ -543,11 +548,11 @@
         force[...] = jnp.sum(yt[...].astype(F32) * acc[...], axis=0, keepdims=True)
 
 
-def field_call(device, codes, even, odd, xt, yt, steps, rows, count, sine):
+def field_call(device, codes, even, odd, xt, yt, steps, rows, count, sine, half=False):
     lines, total = yt.shape
     zeros = (0,) * codes.ndim
     return pl.pallas_call(
-        functools.partial(field_kernel, steps=steps, rows=rows, count=count, sine=sine),
+        functools.partial(field_kernel, steps=steps, rows=rows, count=count, sine=sine, by_half=half),
         grid=(PARTS,),
         in_specs=[
             pl.BlockSpec(memory_space=pltpu.SMEM),
@@ -586,10 +591,27 @@
     return jnp.maximum(high - jnp.maximum(rel, low), 0.0)
 
 
-def local_kernel(device, cells, xt, yt, sums, dens, *, rows, count):
+def unpack(first, second):
+    turn = M.bit_length() - 1
+    first = first.astype(jnp.int32)
+    second = second.astype(jnp.int32)
+    row = (first & (M - 1)).astype(F32)
+    region = (first >> turn) & (REGIONS - 1)
+    height = ((first >> (turn + 2)) + 1).astype(F32)
+    return row, region, height, second & (M - 1), ((second >> turn) + 1).astype(F32)
+
+
+def local_kernel(device, everyone, xt, yt, sums, *, rows, count, cell_count):
     step = pl.program_id(0)
-    total = cells.shape[1]
-    chunk = 512
+    chunk = everyone.shape[2]
+    pieces = 2 * cell_count
+    slab = device[0] >> (cell_count.bit_length() - 1)
+    member = device[0] & (cell_count - 1)
+
+    def source(piece):
+        if piece < cell_count:
+            return slab * cell_count + ((member + piece) & (cell_count - 1))
+        return jnp.maximum(slab - 1, 0) * cell_count + piece - cell_count
 
     @pl.when(step == 0)
     def _():
@@ -597,19 +619,25 @@
         inside = line & (rows - 1)
         place = jnp.where(device[0] >= count // 2, rows - 1 - inside, inside) + device[0] * rows
         place = place.astype(F32)
-        region = (line >> (rows.bit_length() - 1)).astype(F32)
-        for start in range(0, total, chunk):
-            here = pl.ds(start, chunk)
-            value = profile(place - cells[0:1, here], cells[6:7, here], cells[3:4, here])
-            yt[:, here] = jnp.where(region == cells[4:5, here], value, 0.0).astype(BF)
+        owner = line >> (rows.bit_length() - 1)
+        reached = jnp.where((member == 0) & (slab > 0), 0, REGIONS)
+        for piece in range(pieces):
+            cell = everyone[source(piece)]
+            row, region, height, _, _ = unpack(cell[0:1], cell[1:2])
+            if piece >= cell_count:
+                region = region + reached
+            value = profile(place - row, cell[3:4], height)
+            yt[:, pl.ds(piece * chunk, chunk)] = jnp.where(owner == region, value, 0.0).astype(BF)
         sums[...] = jnp.zeros((16, 128), F32)
 
     place = (step % PARTS) * TILE + lax.broadcasted_iota(jnp.int32, (TILE, 1), 0)
     place = jnp.where(step >= PARTS, M - 1 - place, place).astype(F32)
     acc = None
-    for start in range(0, total, chunk):
-        here = pl.ds(start, chunk)
-        value = profile(place - cells[1:2, here], cells[5:6, here], cells[2:3, here]).astype(BF)
+    for piece in range(pieces):
+        here = pl.ds(piece * chunk, chunk)
+        cell = everyone[source(piece)]
+        _, _, _, col, width = unpack(cell[0:1], cell[1:2])
+        value = profile(place - col.astype(F32), cell[2:3], width).astype(BF)
         xt[:, here] = value
         part = lax.dot_general(
             yt[:, here], value, (((1,), (1,)), ((), ())), preferred_element_type=F32
@@ -619,16 +647,16 @@
     sums[8:16, :] += fold_rows(acc)
 
 
-def local_call(device, cells, rows, count):
-    total = cells.shape[1]
+def local_call(device, everyone, rows, count, cell_count):
+    total = 2 * cell_count * everyone.shape[2]
     lines = REGIONS * rows
     whole = lambda t: (0, 0)
     return pl.pallas_call(
-        functools.partial(local_kernel, rows=rows, count=count),
+        functools.partial(local_kernel, rows=rows, count=count, cell_count=cell_count),
         grid=(2 * PARTS,),
         in_specs=[
             pl.BlockSpec(memory_space=pltpu.SMEM),
-            pl.BlockSpec((8, total), whole),
+            pl.BlockSpec(everyone.shape, lambda t: (0, 0, 0)),
         ],
         out_specs=[
             pl.BlockSpec((TILE, total), lambda t: (t, 0)),
@@ -640,24 +668,28 @@
             jax.ShapeDtypeStruct((lines, total), BF),
             jax.ShapeDtypeStruct((16, 128), F32),
         ],
-        scratch_shapes=[pltpu.VMEM((8, 128), F32)],
         compiler_params=params(),
         cost_estimate=pl.CostEstimate(
             flops=2 * lines * M * total, transcendentals=0, bytes_accessed=1 << 23
         ),
         name="local",
-    )(device, cells)
-
-
-SPAN = 256
+    )(device, everyone)
+
+
+BATCH = 2
+BIG = 512
+BIG_PARTS = HALF // BIG
+NEAR = 32
+LOOK = 64
 EXTRA = 16
+DIGIT = 2048.0
+SCALAR_STEPS = steps_of(2.0**36)
 
 
 def spectral_kernel(
     device,
     cells,
-    far_table,
-    near_table,
+    look_table,
     ce_hi,
     ce_lo,
     co_hi,
@@ -671,9 +703,7 @@
     dyo_lo,
     energy,
     dens,
-    far_hi,
-    far_lo,
-    near_both,
+    look,
     even_hi,
     even_lo,
     odd_hi,
@@ -685,9 +715,11 @@
     *,
     slab_count,
     count,
+    batch,
     back_steps,
 ):
     step = pl.program_id(0)
+    cell_steps = slab_count // batch
     slab_rows = M // slab_count
     group = count // 2
     rows = M // count
@@ -700,19 +732,17 @@
     @pl.when(step == 0)
     def _():
         dens[...] = jnp.zeros(dens.shape, F32)
-        far_hi[...], far_lo[...] = split(far_table[...])
-        near_both[:, : SPAN // 2], near_both[:, SPAN // 2 :] = split(near_table[...])
+        look[:, : 2 * LOOK], look[:, 2 * LOOK :] = split(look_table[...])
         energy[...] = jnp.zeros((8, 128), F32)
 
-    @pl.when(step < slab_count)
-    def _():
-        top = step >= slab_count // 2
+    def add_slab(slab, pieces):
+        top = slab >= slab_count // 2
         line = lax.broadcasted_iota(jnp.int32, (window, 1), 0)
-        line = jnp.where(top, window - 1 - line, line) + step * slab_rows
+        line = jnp.where(top, window - 1 - line, line) + slab * slab_rows
         line = line.astype(F32)
         turn = M.bit_length() - 1
         acc = None
-        for piece in range(cells.shape[0]):
+        for piece in pieces:
             first = cells[piece, 0:1, :].astype(jnp.int32)
             second = cells[piece, 1:2, :].astype(jnp.int32)
             low_x = cells[piece, 2:3, :]
@@ -727,31 +757,37 @@
             stacked = jnp.concatenate(
                 [jnp.where(region == g, value_y, 0.0).astype(BF) for g in range(REGIONS)], axis=0
             )
-            head = profile(jnp.zeros_like(low_x), low_x, width_x)
-            tail = profile(width_x, low_x, width_x)
-            base = (col & 7) * 16
-            slot = lax.broadcasted_iota(jnp.int32, (SPAN // 2, 1), 0)
-            feature = jnp.where(slot == base + wide, 1.0, jnp.where(slot == base + 8 + wide, tail, 0.0))
-            feature = jnp.where(slot == base, head, feature).astype(BF)
-            spot = lax.broadcasted_iota(jnp.int32, (SPAN, 1), 0)
-            chosen = jnp.where(spot == (col >> 3), 1.0, 0.0).astype(BF)
-            near = dot(near_both[...], jnp.concatenate([feature, feature], axis=0))
-            far = dot(far_hi[...], chosen) + dot(far_lo[...], chosen)
-            value = near[:width] * far[:width] - near[width:] * far[width:]
+            slot = lax.broadcasted_iota(jnp.int32, (NEAR + 16, 1), 0).astype(F32)
+            inside = (col & (NEAR - 1)).astype(F32)
+            feature = profile(slot - inside, low_x, width_x).astype(BF)
+            feature = jnp.concatenate(
+                [feature, jnp.zeros((LOOK - NEAR - 16, feature.shape[1]), BF)], axis=0
+            )
+            spot = lax.broadcasted_iota(jnp.int32, (LOOK, 1), 0)
+            chosen = jnp.where(spot == (col >> (NEAR.bit_length() - 1)), 1.0, 0.0).astype(BF)
+            found = dot(look[...], jnp.concatenate([feature, chosen, feature, chosen], axis=0))
+            value = found[:width] * found[2 * width : 3 * width]
+            value = value - found[width : 2 * width] * found[3 * width :]
             value = jnp.concatenate(split(value), axis=0)
             part = lax.dot_general(
                 stacked, value, (((1,), (1,)), ((), ())), preferred_element_type=F32
             )
             acc = part if acc is None else acc + part
         half = jnp.where(top, 1, 0)
-        start = jnp.where(top, slab_count - 1 - step, step) * slab_rows
+        start = jnp.where(top, slab_count - 1 - slab, slab) * slab_rows
         here = pl.ds(pl.multiple_of(start, 8), window)
         for g in range(REGIONS):
             lines = slice(g * window, (g + 1) * window)
             lanes = pl.ds(g * width, width)
             dens[half, here, lanes] += acc[lines, :width] + acc[lines, width:]
 
-    @pl.when(step == slab_count)
+    @pl.when(step < cell_steps)
+    def _():
+        share = count // slab_count
+        for inner in range(batch):
+            add_slab(step * batch + inner, range(inner * share, (inner + 1) * share))
+
+    @pl.when(step == cell_steps)
     def _():
         sub = 7 - lax.broadcasted_iota(jnp.int32, (8, 128), 0)
         for tile in range(dens.shape[2] // 128):
@@ -765,87 +801,102 @@
             even_hi[here, :], even_lo[here, :] = split(near + mirrored)
             odd_hi[here, :], odd_lo[here, :] = split(near - mirrored)
 
-    @pl.when((step >= slab_count) & (step < slab_count + PARTS))
-    def _():
-        turn = step - slab_count
+    @pl.when((step >= cell_steps) & (step < cell_steps + BIG_PARTS))
+    def _():
+        turn = step - cell_steps
         unit = math.pi / M
-        lane = lax.broadcasted_iota(jnp.int32, (1, REGIONS * width), 1) & (width - 1)
+        lane = lax.broadcasted_iota(jnp.int32, (1, width), 1)
         odd = jnp.where(member >= group // 2, 1, 0)
         q = (2 * (width * (member - odd * (group // 2)) + lane) + odd).astype(F32)
-        first = lax.broadcasted_iota(jnp.int32, (TILE, 1), 0) + turn * TILE
-        here = pl.ds(pl.multiple_of(turn * TILE, TILE), TILE)
-
-        def solve(spectrum, p):
+        first = lax.broadcasted_iota(jnp.int32, (BIG, 1), 0) + turn * BIG
+        here = pl.ds(pl.multiple_of(turn * BIG, BIG), BIG)
+        spent = jnp.zeros((8, 128), F32)
+
+        def solve(spectrum, p, x_hi, x_lo, y_hi, y_lo, sign_x, sign_y, spent):
             squared = p * p + q * q
             inverse = jnp.where(squared == 0.0, 0.0, 1.0 / jnp.where(squared == 0.0, 1.0, squared))
-            scaled = spectrum * inverse
-            return scaled * (q * (1.0 / unit)), scaled * (p * (1.0 / unit)), spectrum * scaled
+            factor_x = inverse * (q * (sign_x / unit))
+            factor_y = inverse * (p * (sign_y / unit))
+            for g in range(REGIONS):
+                lanes = pl.ds(g * width, width)
+                part = spectrum[:, g * width : (g + 1) * width]
+                x_hi[here, lanes], x_lo[here, lanes] = split(part * factor_x)
+                y_hi[:, lanes], y_lo[:, lanes] = split(part * factor_y)
+                spent = spent + fold_rows(part * (part * inverse))
+            return spent
 
         spec = dot3(ce_hi[...], ce_lo[...], even_hi[...], even_lo[...])
-        drive_x, drive_y, power = solve(spec, (2 * first).astype(F32))
-        dxe_hi[here, :], dxe_lo[here, :] = split(drive_x)
-        dye_hi[...], dye_lo[...] = split(drive_y * sign)
+        spent = solve(
+            spec, (2 * first).astype(F32), dxe_hi, dxe_lo, dye_hi, dye_lo, 1.0, sign, spent
+        )
         spec = dot3(co_hi[...], co_lo[...], odd_hi[...], odd_lo[...])
-        drive_x, drive_y, more = solve(spec, (2 * first + 1).astype(F32))
-        dxo_hi[here, :], dxo_lo[here, :] = split(drive_x * sign)
-        dyo_hi[...], dyo_lo[...] = split(drive_y)
-        energy[...] += fold_rows(power + more) * (1.0 / (unit * unit))
-
-    @pl.when(step >= slab_count + PARTS)
+        spent = solve(
+            spec, (2 * first + 1).astype(F32), dxo_hi, dxo_lo, dyo_hi, dyo_lo, sign, 1.0, spent
+        )
+        energy[...] += spent * (1.0 / (unit * unit))
+
+    @pl.when(step >= cell_steps + BIG_PARTS)
     def _():
         value = dot3(ct_hi[...], ct_lo[...], dxe_hi[...], dxe_lo[...])
         value = value + dot3(co_hi[...], co_lo[...], dxo_hi[...], dxo_lo[...])
-        send_rows(out, (step - slab_count - PARTS) * (TILE // rows), value, upper, back_steps)
-
-
-def send_rows(out, first, value, upper, steps):
-    count, rows = out.shape[0], out.shape[1]
+        first = (step - cell_steps - BIG_PARTS) * (BIG // rows)
+        send_rows(out, first, value, upper, rows, back_steps)
+
+
+def send_rows(out, first, value, upper, rows, steps):
+    count, width = out.shape[0], out.shape[2]
     code = encode(value, steps)
-    for inner in range(TILE // rows):
+    for inner in range(value.shape[0] // rows):
         target = first + inner
         target = jnp.where(upper, count - 1 - target, target)
-        out[target] = code[inner * rows : (inner + 1) * rows]
-
-
-def spectral_call(device, cells, far_table, near_table, tables, slab_count, back_steps):
+        for g in range(REGIONS):
+            here = pl.ds(g * rows, rows)
+            piece = code[inner * rows : (inner + 1) * rows, g * width : (g + 1) * width]
+            out[target, here, :] = piece
+
+
+def spectral_call(device, cells, look_table, tables, slab_count, back_steps):
     fwd_hi, fwd_lo, _, _, ce_hi, ce_lo, _, _ = tables
     count = cells.shape[0]
     group = count // 2
     rows = M // count
     width = M // group
     cols = REGIONS * width
-    share = count // slab_count
-    phase = lambda t: jnp.clip(t - slab_count, 0, PARTS - 1)
-    last = lambda t: jnp.clip(t - slab_count - PARTS, 0, PARTS - 1)
-    both = lambda t: jnp.where(t < slab_count, 0, (t - slab_count) % PARTS)
+    batch = math.gcd(slab_count, BATCH)
+    cell_steps = slab_count // batch
+    share = batch * count // slab_count
+    phase = lambda t: jnp.clip(t - cell_steps, 0, BIG_PARTS - 1)
+    last = lambda t: jnp.clip(t - cell_steps - BIG_PARTS, 0, BIG_PARTS - 1)
+    both = lambda t: jnp.where(t < cell_steps, 0, (t - cell_steps) % BIG_PARTS)
     drive = jax.ShapeDtypeStruct((HALF, cols), BF)
     return pl.pallas_call(
         functools.partial(
-            spectral_kernel, slab_count=slab_count, count=count, back_steps=back_steps
+            spectral_kernel,
+            slab_count=slab_count,
+            count=count,
+            batch=batch,
+            back_steps=back_steps,
         ),
-        grid=(slab_count + 2 * PARTS,),
+        grid=(cell_steps + 2 * BIG_PARTS,),
         in_specs=[
             pl.BlockSpec(memory_space=pltpu.SMEM),
             pl.BlockSpec(
-                (share,) + cells.shape[1:], lambda t: (jnp.minimum(t, slab_count - 1), 0, 0)
+                (share,) + cells.shape[1:], lambda t: (jnp.minimum(t, cell_steps - 1), 0, 0)
             ),
-            pl.BlockSpec(far_table.shape, lambda t: (0, 0)),
-            pl.BlockSpec(near_table.shape, lambda t: (0, 0)),
+            pl.BlockSpec(look_table.shape, lambda t: (0, 0)),
         ]
-        + [pl.BlockSpec((TILE, HALF), lambda t: (phase(t), 0))] * 2
-        + [pl.BlockSpec((TILE, HALF), lambda t: (both(t), 1))] * 2
-        + [pl.BlockSpec((TILE, HALF), lambda t: (last(t), 0))] * 2,
-        out_specs=[pl.BlockSpec((group, rows, cols), lambda t: (0, 0, 0))]
-        + [pl.BlockSpec((TILE, cols), lambda t: (phase(t), 0))] * 4
+        + [pl.BlockSpec((BIG, HALF), lambda t: (phase(t), 0))] * 2
+        + [pl.BlockSpec((BIG, HALF), lambda t: (both(t), 1))] * 2
+        + [pl.BlockSpec((BIG, HALF), lambda t: (last(t), 0))] * 2,
+        out_specs=[pl.BlockSpec((group, REGIONS * rows, width), lambda t: (0, 0, 0))]
+        + [pl.BlockSpec((BIG, cols), lambda t: (phase(t), 0))] * 4
         + [pl.BlockSpec((8, 128), lambda t: (0, 0))],
-        out_shape=[jax.ShapeDtypeStruct((group, rows, cols), I16)]
+        out_shape=[jax.ShapeDtypeStruct((group, REGIONS * rows, width), I16)]
         + [drive] * 4
         + [jax.ShapeDtypeStruct((8, 128), F32)],
         scratch_shapes=[
             pltpu.VMEM((2, HALF + EXTRA, cols), F32),
-            pltpu.VMEM((2 * width, SPAN), BF),
-            pltpu.VMEM((2 * width, SPAN), BF),
-            pltpu.VMEM((2 * width, SPAN), BF),
+            pltpu.VMEM((4 * width, 4 * LOOK), BF),
         ]
         + [pltpu.VMEM((HALF, cols), BF)] * 8,
         compiler_params=params(),
@@ -853,60 +904,89 @@
             flops=30 * HALF * HALF * cols, transcendentals=0, bytes_accessed=1 << 24
         ),
         name="spectral",
-    )(device, cells, far_table, near_table, ce_hi, ce_lo, fwd_hi, fwd_lo, fwd_hi, fwd_lo)
+    )(device, cells, look_table, ce_hi, ce_lo, fwd_hi, fwd_lo, fwd_hi, fwd_lo)
 
 
 def sine_half_kernel(
-    device, dye_hi, dye_lo, dyo_hi, dyo_lo, se_hi, se_lo, so_hi, so_lo, out, *, back_steps
+    device,
+    sums,
+    power,
+    dye_hi,
+    dye_lo,
+    dyo_hi,
+    dyo_lo,
+    se_hi,
+    se_lo,
+    so_hi,
+    so_lo,
+    out,
+    *,
+    rows,
+    back_steps,
 ):
+    @pl.when(pl.program_id(0) == 0)
+    def _():
+        def digits(parts):
+            total = jnp.sum(jnp.sum(parts, axis=1, keepdims=True), axis=0, keepdims=True)
+            first = encode_wide(total, SCALAR_STEPS)
+            rest = (total - decode(first.astype(jnp.int32), SCALAR_STEPS)) * DIGIT
+            return [first, encode_wide(rest, SCALAR_STEPS)]
+
+        shape = (EXTRA, out.shape[2])
+        lane = lax.broadcasted_iota(jnp.int32, shape, 1)
+        lane = jnp.where(lax.broadcasted_iota(jnp.int32, shape, 0) == 0, lane, -1)
+        block = jnp.zeros(shape, F32)
+        codes = digits(sums[0:8, :]) + digits(sums[8:16, :])
+        codes = codes + digits(power[...] * (1.0 / (M * M)))
+        for index, code in enumerate(codes):
+            block = jnp.where(lane == index, code, block)
+        block = block.astype(jnp.int32).astype(I16)
+        for target in range(out.shape[0]):
+            out[target, REGIONS * rows : REGIONS * rows + EXTRA, :] = block
+
     value = dot3(se_hi[...], se_lo[...], dye_hi[...], dye_lo[...])
     value = value + dot3(so_hi[...], so_lo[...], dyo_hi[...], dyo_lo[...])
-    first = pl.program_id(0) * (TILE // out.shape[1])
-    send_rows(out, first, value, device[0] >= out.shape[0], back_steps)
-
-
-def sine_half_call(device, drives, tables, group, rows, back_steps):
+    first = pl.program_id(0) * (TILE // rows)
+    send_rows(out, first, value, device[0] >= out.shape[0], rows, back_steps)
+
+
+def sine_half_call(device, sums, power, drives, tables, group, rows, back_steps):
     sy_hi, sy_lo = tables[2], tables[3]
     cols = drives[0].shape[1]
+    shape = (group, REGIONS * rows + EXTRA, cols // REGIONS)
     return pl.pallas_call(
-        functools.partial(sine_half_kernel, back_steps=back_steps),
+        functools.partial(sine_half_kernel, rows=rows, back_steps=back_steps),
         grid=(PARTS,),
-        in_specs=[pl.BlockSpec(memory_space=pltpu.SMEM)]
+        in_specs=[
+            pl.BlockSpec(memory_space=pltpu.SMEM),
+            pl.BlockSpec((16, 128), lambda t: (0, 0)),
+            pl.BlockSpec((8, 128), lambda t: (0, 0)),
+        ]
         + [pl.BlockSpec((HALF, cols), lambda t: (0, 0))] * 4
         + [pl.BlockSpec((TILE, HALF), lambda t: (t, 0))] * 2
         + [pl.BlockSpec((TILE, HALF), lambda t: (t, 1))] * 2,
-        out_specs=pl.BlockSpec((group, rows, cols), lambda t: (0, 0, 0)),
-        out_shape=jax.ShapeDtypeStruct((group, rows, cols), I16),
+        out_specs=pl.BlockSpec(shape, lambda t: (0, 0, 0)),
+        out_shape=jax.ShapeDtypeStruct(shape, I16),
         compiler_params=params(),
         cost_estimate=pl.CostEstimate(
             flops=12 * HALF * HALF * cols, transcendentals=0, bytes_accessed=1 << 23
         ),
         name="sine_half",
-    )(device, *drives, sy_hi, sy_lo, sy_hi, sy_lo)
-
-
-def cell_tables(q):
-    odd = 2 * np.arange(16) + 1
-    moment = np.concatenate([16 * np.arange(SPAN), odd])
-    phase = (q[:, None] * jnp.asarray(moment, jnp.int32)[None, :]) % (4 * M)
-    angle = phase.astype(F32) * (math.pi / (2.0 * M))
-    both = jnp.concatenate([jnp.cos(angle), jnp.sin(angle)], axis=0)
+    )(device, sums, power, *drives, sy_hi, sy_lo, sy_hi, sy_lo)
+
+
+def cell_tables(first_q, width):
+    line = lax.broadcasted_iota(jnp.int32, (2 * width, 2 * LOOK), 0)
+    lane = lax.broadcasted_iota(jnp.int32, (2 * width, 2 * LOOK), 1)
+    q = first_q + 2 * (line & (width - 1))
+    near = lane < LOOK
+    moment = jnp.where(near, 2 * lane + 1, 2 * NEAR * (lane - LOOK))
+    phase = (q * moment + jnp.where(line < width, 0, 3 * M)) & (4 * M - 1)
     weight = jnp.where(q == 0, math.sqrt(1.0 / M), math.sqrt(2.0 / M)).astype(F32)
-    far = both[:, :SPAN] * jnp.concatenate([weight, weight])[:, None]
-    chosen = np.zeros((16, 8, 16), np.float32)
-    for start in range(8):
-        chosen[start, start, 0] = 1.0
-        for wide in range(1, 9):
-            if wide > 1:
-                chosen[start + 1 : start + wide, start, wide - 1] = 1.0
-            chosen[start + wide, start, 7 + wide] = 1.0
-    near = jnp.dot(
-        both[:, SPAN:],
-        jnp.asarray(chosen.reshape(16, SPAN // 2)),
-        precision=lax.Precision.HIGHEST,
-        preferred_element_type=F32,
+    value = jnp.cos(phase.astype(F32) * (math.pi / (2.0 * M)))
+    return jnp.concatenate(
+        [jnp.where(near, value * weight, 0.0), jnp.where(near, 0.0, value)], axis=0
     )
-    return far, near
 
 
 def exchange(blocks, groups=None):
@@ -947,7 +1027,7 @@
         ]
         pieces.append(lax.ppermute(mine, AXES, pairs))
         back_moves.append([(b, a) for a, b in pairs])
-    tables = make_tables()
+    tables = make_tables(jnp.zeros((1,), jnp.int32), 128)[:8]
     cells = jnp.concatenate(pieces, axis=1)
 
     device = device.astype(jnp.int32).reshape(1)
@@ -1002,66 +1082,45 @@
     device = slab * cell_count + member
     rows = M // count
     width = M // group
+    lines = REGIONS * rows
     own = cell_row.shape[0]
     gain = math.sqrt(2.0 / M)
     back_steps = steps_of(gain**3 * own * count * WMAX * HMAX * 1.1 * M / math.pi * 8.5)
     groups = [list(range(group)), list(range(group, count))]
 
-    first = cell_row + M * (cell_region + REGIONS * (cell_height - 1))
-    second = cell_col + M * (cell_width - 1)
-    mine = jnp.concatenate([jnp.stack([first, second]).astype(F32), cell_offset], axis=0)
-    everyone = exchange(jnp.broadcast_to(mine[None], (count,) + mine.shape))
-    tables = make_tables()
+    first = (cell_row + M * (cell_region + REGIONS * (cell_height - 1))).astype(F32)
+    second = (cell_col + M * (cell_width - 1)).astype(F32)
+    kind = lax.broadcasted_iota(jnp.int32, (count, 4, own), 1)
+    mine = jnp.where(kind == 2, cell_offset[0][None, None, :], cell_offset[1][None, None, :])
+    mine = jnp.where(kind == 1, second[None, None, :], mine)
+    mine = jnp.where(kind == 0, first[None, None, :], mine)
+    everyone = exchange(mine)
     within = device % group
     odd = within // (group // 2)
-    q = 2 * (width * (within - odd * (group // 2)) + lax.iota(jnp.int32, width)) + odd
-    far_table, near_table = cell_tables(q)
+    first_q = 2 * width * (within - odd * (group // 2)) + odd
+    tables = make_tables(first_q.astype(jnp.int32).reshape(1), width)
     scalar = device.astype(jnp.int32).reshape(1)
 
-    drive = spectral_call(scalar, everyone, far_table, near_table, tables, slab_count, back_steps)
+    drive = spectral_call(scalar, everyone, tables[8], tables[:8], slab_count, back_steps)
     along_x = exchange(drive[0], groups)
-    sine_part = sine_half_call(scalar, drive[1:5], tables, group, rows, back_steps)
+    xt, yt, sums = local_call(scalar, everyone, rows, count, cell_count)
+    sine_part = sine_half_call(scalar, sums, drive[5], drive[1:5], tables, group, rows, back_steps)
     along_y = exchange(sine_part, groups)
-
-    begin = jnp.maximum(slab - 1, 0) * cell_count
-    below = lax.dynamic_slice_in_dim(everyone, begin, cell_count)
-    level = lax.dynamic_slice_in_dim(everyone, slab * cell_count, cell_count)
-    near_cells = jnp.concatenate([level, below], axis=0)
-    low = near_cells[:, 0].astype(jnp.int32)
-    wide = near_cells[:, 1].astype(jnp.int32)
-    turn = M.bit_length() - 1
-    block = lax.iota(jnp.int32, 2 * cell_count)[:, None]
-    used = (block < cell_count) | ((member == 0) & (slab > 0))
-    used = used.astype(F32)
-    region = (low >> turn) & (REGIONS - 1)
-    region = jnp.where(used > 0.0, region, REGIONS)
-    fields = [
-        (low & (M - 1)).astype(F32),
-        (wide & (M - 1)).astype(F32),
-        ((wide >> turn) + 1).astype(F32),
-        ((low >> (turn + 2)) + 1).astype(F32),
-        region.astype(F32),
-        near_cells[:, 2],
-        near_cells[:, 3],
-        near_cells[:, 3],
-    ]
-    cells = jnp.stack(fields).reshape(8, 2 * cell_count * own)
-    xt, yt, sums = local_call(scalar, cells, rows, count)
-
-    sums = jnp.concatenate([sums, drive[5]], axis=0)
-    reach = 1
-    while reach < count:
-        sums = sums + lax.ppermute(sums, AXES, [(i, i ^ reach) for i in range(count)])
-        reach *= 2
-    sums = jnp.sum(sums.reshape(3, 8 * 128), axis=1)
+    scalars = jnp.sum(decode(along_y[:, lines : lines + 8, :], SCALAR_STEPS), axis=0)
+    other = lax.ppermute(scalars, AXES, [(i, (i + group) % count) for i in range(count)])
+    joint = scalars[0] + other[0]
 
     fwd, sy, ce, se = tables[0:2], tables[2:4], tables[4:6], tables[6:8]
-    field_x, force_x = field_call(scalar, along_x, se, sy, xt, yt, back_steps, rows, count, True)
-    field_y, force_y = field_call(scalar, along_y, ce, fwd, xt, yt, back_steps, rows, count, False)
+    field_x, force_x = field_call(
+        scalar, along_x, se, sy, xt, yt, back_steps, rows, count, True, True
+    )
+    field_y, force_y = field_call(
+        scalar, along_y, ce, fwd, xt, yt, back_steps, rows, count, False, True
+    )
     partial = jnp.concatenate([force_x, force_y], axis=0).reshape(2, 2 * cell_count, own)
-    cell_force = lax.dynamic_index_in_dim(partial, member, 1, keepdims=False)
+    cell_force = partial[:, 0]
     for turn in range(1, cell_count):
-        piece = lax.dynamic_index_in_dim(partial, (member + turn) % cell_count, 1, keepdims=False)
+        piece = partial[:, turn]
         pairs = [
             (s * cell_count + c, s * cell_count + (c + turn) % cell_count)
             for s in range(slab_count)
@@ -1071,8 +1130,8 @@
     for c in range(cell_count):
         pairs = [(s * cell_count, (s - 1) * cell_count + c) for s in range(1, slab_count)]
         cell_force = cell_force + lax.ppermute(partial[:, cell_count + c], AXES, pairs)
-    energy = sums[2] / (2 * M * M)
-    overflow = sums[0] / sums[1]
+    energy = scalars[0, 4] + scalars[0, 5] * (1.0 / DIGIT)
+    overflow = (joint[0] + joint[1] * (1.0 / DIGIT)) / (joint[2] + joint[3] * (1.0 / DIGIT))
     shape = (REGIONS, rows, M)
     return (field_x.reshape(shape), field_y.reshape(shape), cell_force, energy, overflow)
 

time: 176 us -> 135 us (0.77); the launches traced: 173 us -> 134 us
  blocking collectives: 21.2 us -> 0 us
  waiting for transfers between devices: 10.6 us -> 2.72 us
  Pallas kernels: 103 us -> 96.6 us
  other arithmetic: 6.17 us -> 2.93 us
  local copies, waits for them, and re-layouts: 5.43 us -> 2.69 us
  between operations: 5.11 us -> 6.98 us
    all_to_all x1 -> x0, blocking collectives: 21.2 us -> none  [exchange(): lax.all_to_all(blocks, AXES, split_axis=0, concat_axis=0, tiled=True, axi...]
    ppermute x5 -> x1, waiting for transfers between devices: 9.65 us -> 0.01 us  [half_work(): lax.ppermute(scalars, AXES, [(i, (i + group) % count) for i in range(coun...]
    pallas_call x1, Pallas kernels: 43.8 us -> 35.9 us  [spectral_call(): pl.pallas_call(functools.partial(spectral_kernel, slab_count=slab_count,...]
    all_to_all x2 -> x3, starting transfers between devices: 11.2 us -> 17.4 us  [exchange(): lax.all_to_all(blocks, AXES, split_axis=0, concat_axis=0, tiled=True, axi...]
    ppermute x5 -> x1, starting transfers between devices: 7.21 us -> 2.53 us  [half_work(): lax.ppermute(scalars, AXES, [(i, (i + group) % count) for i in range(coun...]
    all_to_all x2 -> x3, waiting for transfers between devices: 0.01 us -> 2.71 us  [exchange(): lax.all_to_all(blocks, AXES, split_axis=0, concat_axis=0, tiled=True, axi...]
  transfers between devices with their start and end apart: 10 -> 7, of which waited for: 6 -> 1; matrix products, arithmetic and copies ran while one was open for 4% -> 1% of each run, Pallas kernels for 19% -> 45%
where the time goes in v2:
time: 135 us; the launch traced here: 134 us
  Pallas kernels  96.6 us (72%)
  starting transfers between devices  21.9 us (16%)
  between operations  6.98 us (5%)
  other arithmetic  2.93 us (2%)
  waiting for transfers between devices  2.72 us (2%)
  local copies, waits for them, and re-layouts  2.69 us (2%)
    pallas_call x1, Pallas kernels, spectral_call(): pl.pallas_call(functools.partial(spectral_kernel, slab_count=slab_count,...  35.9 us
    pallas_call x2, Pallas kernels, field_call(): pl.pallas_call(functools.partial(field_kernel, steps=steps, rows=rows, co...  28.3 us
    all_to_all x3, starting transfers between devices, exchange(): lax.all_to_all(blocks, AXES, split_axis=0, concat_axis=0, tiled=True, axi...  17.4 us
    pallas_call x1, Pallas kernels, sine_half_call(): pl.pallas_call(functools.partial(sine_half_kernel, rows=rows, back_steps=...  12 us
    pallas_call x1, Pallas kernels, make_tables(): pl.pallas_call(table_kernel, grid=(HALF // (BAND * STRIP),), in_specs=[pl...  11.3 us
    pallas_call x1, Pallas kernels, local_call(): pl.pallas_call(functools.partial(local_kernel, rows=rows, count=count, ce...  9.12 us
    all_to_all x3, waiting for transfers between devices, exchange(): lax.all_to_all(blocks, AXES, split_axis=0, concat_axis=0, tiled=True, axi...  2.71 us
  transfers between devices with their start and end apart: 7, of which 1 were waited for; matrix products, arithmetic and copies ran while one was open for 1% of the time, Pallas kernels for 45%

profile of v2, /device:TPU:0, one launch (start us, length us, event | category | flops | bytes accessed | tf_op | source)
XLA Modules:
  0.0 133.8 jit_solution(5271065366459900158)
XLA Ops:
  0.7 0.8 fusion.5
  1.4 0.8 add_convert_fusion
  2.2 0.8 select_select_fusion
  3.0 7.3 %all-to-all-start = ((f32[32,4,512]{2,1,0:T(4,128)}), f32[32,4,512]{2,1,0:T(4,128)S(1)}, u32[]{:S(2)}, u32[]{:S(2)}) async-start(f32[32,4,512]{2,1,0:T(4,128)} %select_select_fusion), calls=%async_computation | async-start | bytes 524288 | tf_op jit(solution)/shard_map/all_to_all | solution.py:993
  10.4 11.3 %tables.1 = (bf16[1024,2048]{1,0:T(8,128)(2,1)}, bf16[1024,2048]{1,0:T(8,128)(2,1)}, bf16[1024,2048]{1,0:T(8,128)(2,1)}, bf16[1024,2048]{1,0:T(8,128)(2,1)}, bf1...) custom-call(s32[1]{0:T(128)} %bitcast.3.device, ...), custom_call_target="tpu_custom_call" | custom-call | flops 41943040 | bytes 25165824 | tf_op jit(solution)/shard_map/tables/pallas_call | solution.py:155
  21.7 0.0 all-to-all-done.cells.everyone
  21.7 0.0 copy-start.2
  21.7 0.7 copy-done.2
  22.4 35.9 %spectral.1 = (s16[16,256,128]{2,1,0:T(8,128)(2,1)}, bf16[1024,512]{1,0:T(8,128)(2,1)}, bf16[1024,512]{1,0:T(8,128)(2,1)}, bf16[1024,512]{1,0:T(8,128)(2,1)}, bf...) custom-call(s32[1]{0:T(128)} %bitcast.device, f32[32,4,512]{2,1,0:T(4,128)} %copy-done.2, ...), custom_call_target="tpu_custom_call" | custom-call | flops 16106127360 | bytes 16777216 | tf_op jit(solution)/shard_map/spectral/pallas_call | solution.py:872
  58.3 5.0 %all-to-all-start.1 = ((s16[16,256,128]{2,1,0:T(8,128)(2,1)}), s16[16,256,128]{2,1,0:T(8,128)(2,1)S(1)}, u32[]{:S(2)}, u32[]{:S(2)}) async-start(s16[16,256,128]{2,1,0:T(8,128)(2,1)} %get-tuple-element.32), calls=%async_computation.1 | async-start | bytes 2097152 | tf_op jit(solution)/shard_map/all_to_all | solution.py:993
  63.3 9.1 %local.1 = (bf16[2048,2048]{1,0:T(8,128)(2,1)}, bf16[256,2048]{1,0:T(8,128)(2,1)}, f32[16,128]{1,0:T(8,128)}) custom-call(s32[1]{0:T(128)} %bitcast.device, f32[32,4,512]{2,1,0:T(4,128)} %copy-done.2), custom_call_target="tpu_custom_call" | custom-call | flops 2147483648 | bytes 8388608 | tf_op jit(solution)/shard_map/local/pallas_call | solution.py:654
  72.4 12.0 %sine_half.1 = s16[16,272,128]{2,1,0:T(8,128)(2,1)} custom-call(s32[1]{0:T(128)} %bitcast.device, f32[16,128]{1,0:T(8,128)} %get-tuple-element.40.sums, f32[8,128]{1,0:T(8,128)} %get-tuple-element.41.power, bf16[1024,512]{1,0:T(8,128)(2,1)} %get-tuple-element.42.dye_hi, bf16[1024,512]{1,0:T(8,128)(2,1)} %get-tuple-element.43.dye_lo, ...), custom_call_target="tpu_custom_call" | custom-call | flops 6442450944 | bytes 8388608 | tf_op jit(solution)/shard_map/sine_half/pallas_call | solution.py:957
  84.4 0.0 all-to-all-done.1.codes
  84.4 0.0 copy-start.1
  84.4 5.1 %all-to-all-start.2 = ((s16[16,272,128]{2,1,0:T(8,128)(2,1)}), s16[16,272,128]{2,1,0:T(8,128)(2,1)S(1)}, u32[]{:S(2)}, u32[]{:S(2)}) async-start(s16[16,272,128]{2,1,0:T(8,128)(2,1)} %sine_half.1), calls=%async_computation.2 | async-start | bytes 2228224 | tf_op jit(solution)/shard_map/all_to_all | solution.py:993
  89.5 0.0 copy-done.1
  89.6 14.1 %field_x.1 = (f32[256,2048]{1,0:T(8,128)}, f32[1,2048]{1,0:T(1,128)}) custom-call(s32[1]{0:T(128)} %bitcast.device, s16[16,256,128]{2,1,0:T(8,128)(2,1)} %copy-done.1, bf16[1024,1024]{1,0:T(8,128)(2,1)} %get-tuple-element.33.even_hi, bf16[1024,1024]{1,0:T(8,128)(2,1)} %get-tuple-element.34.even_lo, bf16[1024,2048]{1,0:T(8,128)(2,1)} %get-tuple-element.35.odd_hi.se_hi.so_hi, ...), custom_call_target="tpu_custom_call" | custom-call | flops 5368709120 | bytes 16777216 | tf_op jit(solution)/shard_map/field_x/pallas_call | solution.py:554
  103.7 2.7 %all-to-all-done.2.codes = s16[16,272,128]{2,1,0:T(8,128)(2,1)S(1)} async-done(((s16[16,272,128]{2,1,0:T(8,128)(2,1)}), s16[16,272,128]{2,1,0:T(8,128)(2,1)S(1)}, u32[]{:S(2)}, u32[]{:S(2)}) %all-to-all-start.2) | async-done | bytes 1114144 | tf_op jit(solution)/shard_map/all_to_all | solution.py:993
  106.4 0.0 copy-start
  106.4 0.0 copy-start.3
  106.4 2.5 %collective-permute-start.3 = (f32[8,128]{1,0:T(8,128)S(1)}, f32[8,128]{1,0:T(8,128)S(1)}, u32[]{:S(2)}, u32[]{:S(2)}) collective-permute-start(f32[8,128]{1,0:T(8,128)S(1)} %fusion), channel_id=1, source_target_pairs={{0,16},{1,17},{2,18},{3,19},{4,20},{5,21},{6,22},{7,23},{8,24},{9,... | collective-permute-start | bytes 12296 | tf_op jit(solution)/shard_map/ppermute | solution.py:1110
  109.0 0.0 copy-done
  109.0 14.1 %field_y.1 = (f32[256,2048]{1,0:T(8,128)}, f32[1,2048]{1,0:T(1,128)}) custom-call(s32[1]{0:T(128)} %bitcast.device, s16[16,272,128]{2,1,0:T(8,128)(2,1)} %copy-done, bf16[1024,1024]{1,0:T(8,128)(2,1)} %get-tuple-element.28.ce_hi.even_hi, bf16[1024,1024]{1,0:T(8,128)(2,1)} %get-tuple-element.29.ce_lo.even_lo, ...), custom_call_target="tpu_custom_call" | custom-call | flops 5368709120 | bytes 16777216 | tf_op jit(solution)/shard_map/field_y/pallas_call | solution.py:554
  123.1 0.0 copy-done.3
  123.1 0.7 pad_maximum_fusion
  123.8 0.6 fusion.4
  124.4 0.0 collective-permute-start
  124.4 1.3 collective-permute-start.1
  125.7 0.7 collective-permute-start.2
  127.7 0.0 collective-permute-done.3
  127.7 0.6 fusion.6
  130.9 0.0 collective-permute-done
  130.9 0.0 collective-permute-done.1
  130.9 0.0 collective-permute-done.2
  131.0 0.6 fusion.3
  (5 shorter events, 0.1 us)
Async XLA Ops:
  3.0 18.7 %all-to-all-start = ((f32[32,4,512]{2,1,0:T(4,128)}), f32[32,4,512]{2,1,0:T(4,128)S(1)}, u32[]{:S(2)}, u32[]{:S(2)}) async-start(f32[32,4,512]{2,1,0:T(4,128)} %select_select_fusion), calls=%async_computation | async-start | bytes 524288 | tf_op jit(solution)/shard_map/all_to_all | solution.py:993
  21.7 0.7 copy-start.2
  58.3 26.1 %all-to-all-start.1 = ((s16[16,256,128]{2,1,0:T(8,128)(2,1)}), s16[16,256,128]{2,1,0:T(8,128)(2,1)S(1)}, u32[]{:S(2)}, u32[]{:S(2)}) async-start(s16[16,256,128]{2,1,0:T(8,128)(2,1)} %get-tuple-element.32), calls=%async_computation.1 | async-start | bytes 2097152 | tf_op jit(solution)/shard_map/all_to_all | solution.py:993
  84.4 5.1 %copy-start.1 = (s16[16,256,128]{2,1,0:T(8,128)(2,1)}, s16[16,256,128]{2,1,0:T(8,128)(2,1)S(1)}, u32[]{:S(2)}) copy-start(s16[16,256,128]{2,1,0:T(8,128)(2,1)S(1)} %all-to-all-done.1.codes) | copy-start | bytes 3145732
  84.4 22.0 %all-to-all-start.2 = ((s16[16,272,128]{2,1,0:T(8,128)(2,1)}), s16[16,272,128]{2,1,0:T(8,128)(2,1)S(1)}, u32[]{:S(2)}, u32[]{:S(2)}) async-start(s16[16,272,128]{2,1,0:T(8,128)(2,1)} %sine_half.1), calls=%async_computation.2 | async-start | bytes 2228224 | tf_op jit(solution)/shard_map/all_to_all | solution.py:993
  106.4 2.6 %copy-start = (s16[16,272,128]{2,1,0:T(8,128)(2,1)}, s16[16,272,128]{2,1,0:T(8,128)(2,1)S(1)}, u32[]{:S(2)}) copy-start(s16[16,272,128]{2,1,0:T(8,128)(2,1)S(1)} %all-to-all-done.2.codes) | copy-start | bytes 3342340
  106.4 16.7 %copy-start.3 = (f32[1,2048]{1,0:T(1,128)S(1)}, f32[1,2048]{1,0:T(1,128)}, u32[]{:S(2)}) copy-start(f32[1,2048]{1,0:T(1,128)} %get-tuple-element.47) | copy-start | bytes 24580
  106.4 21.3 %collective-permute-start.3 = (f32[8,128]{1,0:T(8,128)S(1)}, f32[8,128]{1,0:T(8,128)S(1)}, u32[]{:S(2)}, u32[]{:S(2)}) collective-permute-start(f32[8,128]{1,0:T(8,128)S(1)} %fusion), channel_id=1, source_target_pairs={{0,16},{1,17},{2,18},{3,19},{4,20},{5,21},{6,22},{7,23},{8,24},{9,... | collective-permute-start | bytes 12296 | tf_op jit(solution)/shard_map/ppermute | solution.py:1110
  124.4 6.5 %collective-permute-start = (f32[2,512]{1,0:T(2,128)S(1)}, f32[2,512]{1,0:T(2,128)S(1)}, u32[]{:S(2)}, u32[]{:S(2)}) collective-permute-start(f32[2,512]{1,0:T(2,128)S(1)} %get-tuple-element.49), channel_id=1, source_target_pairs={{0,1},{1,0},{2,3},{3,2},{4,5},{5,4},{6,7},{7,6},{8,9},{9,8},{10,11... | collective-permute-start | bytes 12296 | tf_op jit(solution)/shard_map/ppermute | solution.py:1129
  124.4 6.5 %collective-permute-start.1 = (f32[2,512]{1,0:T(2,128)S(1)}, f32[2,512]{1,0:T(2,128)S(1)}, u32[]{:S(2)}, u32[]{:S(2)}) collective-permute-start(f32[2,512]{1,0:T(2,128)S(1)} %get-tuple-element.51), channel_id=1, source_target_pairs={{2,0},{4,2},{6,4},{8,6},{10,8},{12,10},{14,12},{16,14},{18,16},{20... | collective-permute-start | bytes 12296 | tf_op jit(solution)/shard_map/ppermute | solution.py:1132
  125.7 5.2 %collective-permute-start.2 = (f32[2,512]{1,0:T(2,128)S(1)}, f32[2,512]{1,0:T(2,128)S(1)}, u32[]{:S(2)}, u32[]{:S(2)}) collective-permute-start(f32[2,512]{1,0:T(2,128)S(1)} %get-tuple-element.50), channel_id=1, source_target_pairs={{2,1},{4,3},{6,5},{8,7},{10,9},{12,11},{14,13},{16,15},{18,17},{20... | collective-permute-start | bytes 12296 | tf_op jit(solution)/shard_map/ppermute | solution.py:1132

commit v3 on v2

--- a/solution.py
+++ b/solution.py
@@ -468,6 +468,7 @@
     x_near,
     x_far,
     yt,
+    earlier,
     field,
     force,
     part_hi,
@@ -545,12 +546,16 @@
 
     @pl.when(step == PARTS - 1)
     def _():
-        force[...] = jnp.sum(yt[...].astype(F32) * acc[...], axis=0, keepdims=True)
-
-
-def field_call(device, codes, even, odd, xt, yt, steps, rows, count, sine, half=False):
+        latest = jnp.sum(yt[...].astype(F32) * acc[...], axis=0, keepdims=True)
+        force[...] = jnp.concatenate([earlier[...], latest], axis=0)[1 - force.shape[0] + 1 :]
+
+
+def field_call(device, codes, even, odd, xt, yt, steps, rows, count, sine, half=False, earlier=None):
     lines, total = yt.shape
     zeros = (0,) * codes.ndim
+    found = 1 if earlier is None else 2
+    if earlier is None:
+        earlier = jnp.zeros((1, total), F32)
     return pl.pallas_call(
         functools.partial(field_kernel, steps=steps, rows=rows, count=count, sine=sine, by_half=half),
         grid=(PARTS,),
@@ -564,14 +569,15 @@
             pl.BlockSpec((TILE, total), lambda t: (t, 0)),
             pl.BlockSpec((TILE, total), lambda t: (PARTS + t, 0)),
             pl.BlockSpec((lines, total), lambda t: (0, 0)),
+            pl.BlockSpec((1, total), lambda t: (0, 0)),
         ],
         out_specs=[
             pl.BlockSpec((lines, M), lambda t: (0, 0)),
-            pl.BlockSpec((1, total), lambda t: (0, 0)),
+            pl.BlockSpec((found, total), lambda t: (0, 0)),
         ],
         out_shape=[
             jax.ShapeDtypeStruct((lines, M), F32),
-            jax.ShapeDtypeStruct((1, total), F32),
+            jax.ShapeDtypeStruct((found, total), F32),
         ],
         scratch_shapes=[
             pltpu.VMEM((2, lines, HALF), BF),
@@ -583,12 +589,28 @@
             flops=2 * lines * M * (total + 3 * HALF), transcendentals=0, bytes_accessed=1 << 24
         ),
         name="field_x" if sine else "field_y",
-    )(device, codes, even[0], even[1], odd[0], odd[1], xt, xt, yt)
+    )(device, codes, even[0], even[1], odd[0], odd[1], xt, xt, yt, earlier)
 
 
 def profile(rel, low, extent):
     high = jnp.minimum(rel + 1.0, low + extent)
     return jnp.maximum(high - jnp.maximum(rel, low), 0.0)
+
+
+def prepare_kernel(row, col, width, height, region, offset, out):
+    first = row[...] + M * (region[...] + REGIONS * (height[...] - 1))
+    second = col[...] + M * (width[...] - 1)
+    block = jnp.concatenate([first.astype(F32), second.astype(F32), offset[...]], axis=0)
+    for target in range(out.shape[0]):
+        out[target] = block
+
+
+def prepare_call(lists, offset, count):
+    return pl.pallas_call(
+        prepare_kernel,
+        out_shape=jax.ShapeDtypeStruct((count, 4, offset.shape[1]), F32),
+        name="prepare",
+    )(*lists, offset)
 
 
 def unpack(first, second):
@@ -630,8 +652,8 @@
             yt[:, pl.ds(piece * chunk, chunk)] = jnp.where(owner == region, value, 0.0).astype(BF)
         sums[...] = jnp.zeros((16, 128), F32)
 
-    place = (step % PARTS) * TILE + lax.broadcasted_iota(jnp.int32, (TILE, 1), 0)
-    place = jnp.where(step >= PARTS, M - 1 - place, place).astype(F32)
+    place = (step % BIG_PARTS) * BIG + lax.broadcasted_iota(jnp.int32, (BIG, 1), 0)
+    place = jnp.where(step >= BIG_PARTS, M - 1 - place, place).astype(F32)
     acc = None
     for piece in range(pieces):
         here = pl.ds(piece * chunk, chunk)
@@ -653,13 +675,13 @@
     whole = lambda t: (0, 0)
     return pl.pallas_call(
         functools.partial(local_kernel, rows=rows, count=count, cell_count=cell_count),
-        grid=(2 * PARTS,),
+        grid=(2 * BIG_PARTS,),
         in_specs=[
             pl.BlockSpec(memory_space=pltpu.SMEM),
             pl.BlockSpec(everyone.shape, lambda t: (0, 0, 0)),
         ],
         out_specs=[
-            pl.BlockSpec((TILE, total), lambda t: (t, 0)),
+            pl.BlockSpec((BIG, total), lambda t: (t, 0)),
             pl.BlockSpec((lines, total), whole),
             pl.BlockSpec((16, 128), whole),
         ],
@@ -676,7 +698,7 @@
     )(device, everyone)
 
 
-BATCH = 2
+BATCH = 4
 BIG = 512
 BIG_PARTS = HALF // BIG
 NEAR = 32
@@ -740,39 +762,29 @@
         line = lax.broadcasted_iota(jnp.int32, (window, 1), 0)
         line = jnp.where(top, window - 1 - line, line) + slab * slab_rows
         line = line.astype(F32)
-        turn = M.bit_length() - 1
-        acc = None
-        for piece in pieces:
-            first = cells[piece, 0:1, :].astype(jnp.int32)
-            second = cells[piece, 1:2, :].astype(jnp.int32)
-            low_x = cells[piece, 2:3, :]
-            low_y = cells[piece, 3:4, :]
-            row = (first & (M - 1)).astype(F32)
-            region = (first >> turn) & (REGIONS - 1)
-            height = ((first >> (turn + 2)) + 1).astype(F32)
-            col = second & (M - 1)
-            wide = second >> turn
-            width_x = (wide + 1).astype(F32)
-            value_y = profile(line - row, low_y, height)
-            stacked = jnp.concatenate(
-                [jnp.where(region == g, value_y, 0.0).astype(BF) for g in range(REGIONS)], axis=0
-            )
-            slot = lax.broadcasted_iota(jnp.int32, (NEAR + 16, 1), 0).astype(F32)
-            inside = (col & (NEAR - 1)).astype(F32)
-            feature = profile(slot - inside, low_x, width_x).astype(BF)
-            feature = jnp.concatenate(
-                [feature, jnp.zeros((LOOK - NEAR - 16, feature.shape[1]), BF)], axis=0
-            )
-            spot = lax.broadcasted_iota(jnp.int32, (LOOK, 1), 0)
-            chosen = jnp.where(spot == (col >> (NEAR.bit_length() - 1)), 1.0, 0.0).astype(BF)
-            found = dot(look[...], jnp.concatenate([feature, chosen, feature, chosen], axis=0))
-            value = found[:width] * found[2 * width : 3 * width]
-            value = value - found[width : 2 * width] * found[3 * width :]
-            value = jnp.concatenate(split(value), axis=0)
-            part = lax.dot_general(
-                stacked, value, (((1,), (1,)), ((), ())), preferred_element_type=F32
-            )
-            acc = part if acc is None else acc + part
+        cell = jnp.concatenate([cells[piece] for piece in pieces], axis=1)
+        row, region, height, col, width_x = unpack(cell[0:1], cell[1:2])
+        low_x, low_y = cell[2:3], cell[3:4]
+        value_y = profile(line - row, low_y, height).astype(BF)
+        stacked = jnp.concatenate(
+            [value_y * jnp.where(region == g, 1.0, 0.0).astype(BF) for g in range(REGIONS)],
+            axis=0,
+        )
+        slot = lax.broadcasted_iota(jnp.int32, (NEAR + 16, 1), 0).astype(F32)
+        inside = (col & (NEAR - 1)).astype(F32)
+        feature = profile(slot - inside, low_x, width_x).astype(BF)
+        feature = jnp.concatenate(
+            [feature, jnp.zeros((LOOK - NEAR - 16, feature.shape[1]), BF)], axis=0
+        )
+        spot = lax.broadcasted_iota(jnp.int32, (LOOK, 1), 0)
+        chosen = jnp.where(spot == (col >> (NEAR.bit_length() - 1)), 1.0, 0.0).astype(BF)
+        found = dot(look[...], jnp.concatenate([feature, chosen, feature, chosen], axis=0))
+        value = found[:width] * found[2 * width : 3 * width]
+        value = value - found[width : 2 * width] * found[3 * width :]
+        value = jnp.concatenate(split(value), axis=0)
+        acc = lax.dot_general(
+            stacked, value, (((1,), (1,)), ((), ())), preferred_element_type=F32
+        )
         half = jnp.where(top, 1, 0)
         start = jnp.where(top, slab_count - 1 - slab, slab) * slab_rows
         here = pl.ds(pl.multiple_of(start, 8), window)
@@ -1088,12 +1100,8 @@
     back_steps = steps_of(gain**3 * own * count * WMAX * HMAX * 1.1 * M / math.pi * 8.5)
     groups = [list(range(group)), list(range(group, count))]
 
-    first = (cell_row + M * (cell_region + REGIONS * (cell_height - 1))).astype(F32)
-    second = (cell_col + M * (cell_width - 1)).astype(F32)
-    kind = lax.broadcasted_iota(jnp.int32, (count, 4, own), 1)
-    mine = jnp.where(kind == 2, cell_offset[0][None, None, :], cell_offset[1][None, None, :])
-    mine = jnp.where(kind == 1, second[None, None, :], mine)
-    mine = jnp.where(kind == 0, first[None, None, :], mine)
+    lists = [cell_row, cell_col, cell_width, cell_height, cell_region]
+    mine = prepare_call([item.reshape(1, own) for item in lists], cell_offset, count)
     everyone = exchange(mine)
     within = device % group
     odd = within // (group // 2)
@@ -1114,13 +1122,12 @@
     field_x, force_x = field_call(
         scalar, along_x, se, sy, xt, yt, back_steps, rows, count, True, True
     )
-    field_y, force_y = field_call(
-        scalar, along_y, ce, fwd, xt, yt, back_steps, rows, count, False, True
+    field_y, partial = field_call(
+        scalar, along_y, ce, fwd, xt, yt, back_steps, rows, count, False, True, force_x
     )
-    partial = jnp.concatenate([force_x, force_y], axis=0).reshape(2, 2 * cell_count, own)
-    cell_force = partial[:, 0]
+    cell_force = partial[:, :own]
     for turn in range(1, cell_count):
-        piece = partial[:, turn]
+        piece = partial[:, turn * own : (turn + 1) * own]
         pairs = [
             (s * cell_count + c, s * cell_count + (c + turn) % cell_count)
             for s in range(slab_count)
@@ -1129,7 +1136,9 @@
         cell_force = cell_force + lax.ppermute(piece, AXES, pairs)
     for c in range(cell_count):
         pairs = [(s * cell_count, (s - 1) * cell_count + c) for s in range(1, slab_count)]
-        cell_force = cell_force + lax.ppermute(partial[:, cell_count + c], AXES, pairs)
+        cell_force = cell_force + lax.ppermute(
+            partial[:, (cell_count + c) * own : (cell_count + c + 1) * own], AXES, pairs
+        )
     energy = scalars[0, 4] + scalars[0, 5] * (1.0 / DIGIT)
     overflow = (joint[0] + joint[1] * (1.0 / DIGIT)) / (joint[2] + joint[3] * (1.0 / DIGIT))
     shape = (REGIONS, rows, M)

time: 135 us -> 133 us (0.985)
  other arithmetic: 2.93 us -> 1.32 us
    pallas_call x1, Pallas kernels: 35.9 us -> 34 us  [spectral_call(): pl.pallas_call(functools.partial(spectral_kernel, slab_count=slab_count,...]
    pallas_call x0 -> x1, Pallas kernels: none -> 1.5 us  [prepare_call(): pl.pallas_call(prepare_kernel, out_shape=jax.ShapeDtypeStruct((count, 4,...]
  transfers between devices with their start and end apart: 7 -> 7, of which waited for: 1 -> 1; matrix products, arithmetic and copies ran while one was open for 1% -> 2% of each run, Pallas kernels for 45% -> 46%
where the time goes in v3:
time: 133 us; the launch traced here: 131 us
  Pallas kernels  95.6 us (72%)
  starting transfers between devices  21.9 us (16%)
  between operations  7.07 us (5%)
  local copies, waits for them, and re-layouts  3.25 us (2%)
  waiting for transfers between devices  2.11 us (2%)
    pallas_call x1, Pallas kernels, spectral_call(): pl.pallas_call(functools.partial(spectral_kernel, slab_count=slab_count,...  34 us
    pallas_call x2, Pallas kernels, field_call(): pl.pallas_call(functools.partial(field_kernel, steps=steps, rows=rows, co...  28.2 us
    all_to_all x3, starting transfers between devices, exchange(): lax.all_to_all(blocks, AXES, split_axis=0, concat_axis=0, tiled=True, axi...  17.4 us
    pallas_call x1, Pallas kernels, sine_half_call(): pl.pallas_call(functools.partial(sine_half_kernel, rows=rows, back_steps=...  12 us
    pallas_call x1, Pallas kernels, make_tables(): pl.pallas_call(table_kernel, grid=(HALF // (BAND * STRIP),), in_specs=[pl...  11.3 us
    pallas_call x1, Pallas kernels, local_call(): pl.pallas_call(functools.partial(local_kernel, rows=rows, count=count, ce...  8.66 us
  transfers between devices with their start and end apart: 7, of which 1 were waited for; matrix products, arithmetic and copies ran while one was open for 2% of the time, Pallas kernels for 46%

profile of v3, /device:TPU:0, one launch (start us, length us, event | category | flops | bytes accessed | tf_op | source)
XLA Modules:
  0.0 131.3 jit_solution(14832482284268355892)
XLA Ops:
  0.6 1.5 %prepare.1 = f32[32,4,512]{2,1,0:T(4,128)} custom-call(s32[1,512]{1,0:T(1,128)} %bitcast.11, s32[1,512]{1,0:T(1,128)} %bitcast.12, s32[1,512]{1,0:T(1,128)} %bitcast.13, s32[1,512]{1,0:T(1,128)} %bitcast.14, s32[1,512]{1,0:T(1,128)} %bitcast.15, f32[2,512]{1,0:T(2,128)} %offset.1), custom_call_target="tpu_custom_call" | custom-call | tf_op jit(solution)/shard_map/prepare/pallas_call | solution.py:609
  2.1 7.3 %all-to-all-start = ((f32[32,4,512]{2,1,0:T(4,128)}), f32[32,4,512]{2,1,0:T(4,128)S(1)}, u32[]{:S(2)}, u32[]{:S(2)}) async-start(f32[32,4,512]{2,1,0:T(4,128)} %prepare.1), calls=%async_computation | async-start | bytes 524288 | tf_op jit(solution)/shard_map/all_to_all | solution.py:1005
  9.5 11.3 %tables.1 = (bf16[1024,2048]{1,0:T(8,128)(2,1)}, bf16[1024,2048]{1,0:T(8,128)(2,1)}, bf16[1024,2048]{1,0:T(8,128)(2,1)}, bf16[1024,2048]{1,0:T(8,128)(2,1)}, bf1...) custom-call(s32[1]{0:T(128)} %bitcast.6.device, ...), custom_call_target="tpu_custom_call" | custom-call | flops 41943040 | bytes 25165824 | tf_op jit(solution)/shard_map/tables/pallas_call | solution.py:155
  20.8 0.0 all-to-all-done.cells.everyone
  20.8 0.0 copy-start.2
  20.8 0.7 copy-done.2
  21.5 34.0 %spectral.1 = (s16[16,256,128]{2,1,0:T(8,128)(2,1)}, bf16[1024,512]{1,0:T(8,128)(2,1)}, bf16[1024,512]{1,0:T(8,128)(2,1)}, bf16[1024,512]{1,0:T(8,128)(2,1)}, bf...) custom-call(s32[1]{0:T(128)} %bitcast.device, f32[32,4,512]{2,1,0:T(4,128)} %copy-done.2, ...), custom_call_target="tpu_custom_call" | custom-call | flops 16106127360 | bytes 16777216 | tf_op jit(solution)/shard_map/spectral/pallas_call | solution.py:884
  55.5 5.0 %all-to-all-start.1 = ((s16[16,256,128]{2,1,0:T(8,128)(2,1)}), s16[16,256,128]{2,1,0:T(8,128)(2,1)S(1)}, u32[]{:S(2)}, u32[]{:S(2)}) async-start(s16[16,256,128]{2,1,0:T(8,128)(2,1)} %get-tuple-element.32), calls=%async_computation.1 | async-start | bytes 2097152 | tf_op jit(solution)/shard_map/all_to_all | solution.py:1005
  60.5 8.7 %local.1 = (bf16[2048,2048]{1,0:T(8,128)(2,1)}, bf16[256,2048]{1,0:T(8,128)(2,1)}, f32[16,128]{1,0:T(8,128)}) custom-call(s32[1]{0:T(128)} %bitcast.device, f32[32,4,512]{2,1,0:T(4,128)} %copy-done.2), custom_call_target="tpu_custom_call" | custom-call | flops 2147483648 | bytes 8388608 | tf_op jit(solution)/shard_map/local/pallas_call | solution.py:676
  69.2 12.0 %sine_half.1 = s16[16,272,128]{2,1,0:T(8,128)(2,1)} custom-call(s32[1]{0:T(128)} %bitcast.device, f32[16,128]{1,0:T(8,128)} %get-tuple-element.40.sums, f32[8,128]{1,0:T(8,128)} %get-tuple-element.41.power, bf16[1024,512]{1,0:T(8,128)(2,1)} %get-tuple-element.42.dye_hi, bf16[1024,512]{1,0:T(8,128)(2,1)} %get-tuple-element.43.dye_lo, ...), custom_call_target="tpu_custom_call" | custom-call | flops 6442450944 | bytes 8388608 | tf_op jit(solution)/shard_map/sine_half/pallas_call | solution.py:969
  81.1 0.0 all-to-all-done.1.codes
  81.1 0.0 copy-start.1
  81.1 5.1 %all-to-all-start.2 = ((s16[16,272,128]{2,1,0:T(8,128)(2,1)}), s16[16,272,128]{2,1,0:T(8,128)(2,1)S(1)}, u32[]{:S(2)}, u32[]{:S(2)}) async-start(s16[16,272,128]{2,1,0:T(8,128)(2,1)} %sine_half.1), calls=%async_computation.2 | async-start | bytes 2228224 | tf_op jit(solution)/shard_map/all_to_all | solution.py:1005
  86.3 0.6 broadcast_in_dim.3.earlier
  86.8 0.0 copy-done.1
  86.9 14.1 %field_x.1 = (f32[256,2048]{1,0:T(8,128)}, f32[1,2048]{1,0:T(1,128)}) custom-call(s32[1]{0:T(128)} %bitcast.device, s16[16,256,128]{2,1,0:T(8,128)(2,1)} %copy-done.1, bf16[1024,1024]{1,0:T(8,128)(2,1)} %get-tuple-element.33.even_hi, bf16[1024,1024]{1,0:T(8,128)(2,1)} %get-tuple-element.34.even_lo, bf16[1024,2048]{1,0:T(8,128)(2,1)} %get-tuple-element.35.odd_hi.se_hi.so_hi, ...), custom_call_target="tpu_custom_call" | custom-call | flops 5368709120 | bytes 16777216 | tf_op jit(solution)/shard_map/field_x/pallas_call | solution.py:559
  101.0 2.1 %all-to-all-done.2.codes = s16[16,272,128]{2,1,0:T(8,128)(2,1)S(1)} async-done(((s16[16,272,128]{2,1,0:T(8,128)(2,1)}), s16[16,272,128]{2,1,0:T(8,128)(2,1)S(1)}, u32[]{:S(2)}, u32[]{:S(2)}) %all-to-all-start.2) | async-done | bytes 1114144 | tf_op jit(solution)/shard_map/all_to_all | solution.py:1005
  103.1 0.0 copy-start
  103.1 2.5 %collective-permute-start.3 = (f32[8,128]{1,0:T(8,128)S(1)}, f32[8,128]{1,0:T(8,128)S(1)}, u32[]{:S(2)}, u32[]{:S(2)}) collective-permute-start(f32[8,128]{1,0:T(8,128)S(1)} %fusion), channel_id=1, source_target_pairs={{0,16},{1,17},{2,18},{3,19},{4,20},{5,21},{6,22},{7,23},{8,24},{9,... | collective-permute-start | bytes 12296 | tf_op jit(solution)/shard_map/ppermute | solution.py:1118
  105.7 0.0 copy-done
  105.7 14.1 %field_y.1 = (f32[256,2048]{1,0:T(8,128)}, f32[2,2048]{1,0:T(2,128)}) custom-call(s32[1]{0:T(128)} %bitcast.device, s16[16,272,128]{2,1,0:T(8,128)(2,1)} %copy-done, bf16[1024,1024]{1,0:T(8,128)(2,1)} %get-tuple-element.28.ce_hi.even_hi, bf16[1024,1024]{1,0:T(8,128)(2,1)} %get-tuple-element.29.ce_lo.even_lo, ...), custom_call_target="tpu_custom_call" | custom-call | flops 5368709120 | bytes 16777216 | tf_op jit(solution)/shard_map/field_y/pallas_call | solution.py:559
  119.8 0.7 fusion.1
  120.4 0.6 fusion.2
  121.0 0.0 collective-permute-start
  121.0 1.3 collective-permute-start.1
  122.3 0.7 collective-permute-start.2
  124.3 0.0 collective-permute-done.3
  124.3 0.7 fusion.3
  127.7 0.0 collective-permute-done
  127.7 0.0 collective-permute-done.1
  127.7 0.0 collective-permute-done.2
  127.7 1.3 add_add_fusion
  (2 shorter events, 0.0 us)
Async XLA Ops:
  2.1 18.7 %all-to-all-start = ((f32[32,4,512]{2,1,0:T(4,128)}), f32[32,4,512]{2,1,0:T(4,128)S(1)}, u32[]{:S(2)}, u32[]{:S(2)}) async-start(f32[32,4,512]{2,1,0:T(4,128)} %prepare.1), calls=%async_computation | async-start | bytes 524288 | tf_op jit(solution)/shard_map/all_to_all | solution.py:1005
  20.8 0.7 copy-start.2
  55.5 25.6 %all-to-all-start.1 = ((s16[16,256,128]{2,1,0:T(8,128)(2,1)}), s16[16,256,128]{2,1,0:T(8,128)(2,1)S(1)}, u32[]{:S(2)}, u32[]{:S(2)}) async-start(s16[16,256,128]{2,1,0:T(8,128)(2,1)} %get-tuple-element.32), calls=%async_computation.1 | async-start | bytes 2097152 | tf_op jit(solution)/shard_map/all_to_all | solution.py:1005
  81.1 5.7 %copy-start.1 = (s16[16,256,128]{2,1,0:T(8,128)(2,1)}, s16[16,256,128]{2,1,0:T(8,128)(2,1)S(1)}, u32[]{:S(2)}) copy-start(s16[16,256,128]{2,1,0:T(8,128)(2,1)S(1)} %all-to-all-done.1.codes) | copy-start | bytes 3145732
  81.1 22.0 %all-to-all-start.2 = ((s16[16,272,128]{2,1,0:T(8,128)(2,1)}), s16[16,272,128]{2,1,0:T(8,128)(2,1)S(1)}, u32[]{:S(2)}, u32[]{:S(2)}) async-start(s16[16,272,128]{2,1,0:T(8,128)(2,1)} %sine_half.1), calls=%async_computation.2 | async-start | bytes 2228224 | tf_op jit(solution)/shard_map/all_to_all | solution.py:1005
  103.1 2.6 %copy-start = (s16[16,272,128]{2,1,0:T(8,128)(2,1)}, s16[16,272,128]{2,1,0:T(8,128)(2,1)S(1)}, u32[]{:S(2)}) copy-start(s16[16,272,128]{2,1,0:T(8,128)(2,1)S(1)} %all-to-all-done.2.codes) | copy-start | bytes 3342340
  103.1 21.2 %collective-permute-start.3 = (f32[8,128]{1,0:T(8,128)S(1)}, f32[8,128]{1,0:T(8,128)S(1)}, u32[]{:S(2)}, u32[]{:S(2)}) collective-permute-start(f32[8,128]{1,0:T(8,128)S(1)} %fusion), channel_id=1, source_target_pairs={{0,16},{1,17},{2,18},{3,19},{4,20},{5,21},{6,22},{7,23},{8,24},{9,... | collective-permute-start | bytes 12296 | tf_op jit(solution)/shard_map/ppermute | solution.py:1118
  121.0 6.7 %collective-permute-start = (f32[2,512]{1,0:T(2,128)S(1)}, f32[2,512]{1,0:T(2,128)S(1)}, u32[]{:S(2)}, u32[]{:S(2)}) collective-permute-start(f32[2,512]{1,0:T(2,128)S(1)} %get-tuple-element.49), channel_id=1, source_target_pairs={{0,1},{1,0},{2,3},{3,2},{4,5},{5,4},{6,7},{7,6},{8,9},{9,8},{10,11... | collective-permute-start | bytes 12296 | tf_op jit(solution)/shard_map/ppermute | solution.py:1136
  121.0 6.7 %collective-permute-start.1 = (f32[2,512]{1,0:T(2,128)S(1)}, f32[2,512]{1,0:T(2,128)S(1)}, u32[]{:S(2)}, u32[]{:S(2)}) collective-permute-start(f32[2,512]{1,0:T(2,128)S(1)} %get-tuple-element.51), channel_id=1, source_target_pairs={{2,0},{4,2},{6,4},{8,6},{10,8},{12,10},{14,12},{16,14},{18,16},{20... | collective-permute-start | bytes 12296 | tf_op jit(solution)/shard_map/ppermute | solution.py:1139
  122.3 5.4 %collective-permute-start.2 = (f32[2,512]{1,0:T(2,128)S(1)}, f32[2,512]{1,0:T(2,128)S(1)}, u32[]{:S(2)}, u32[]{:S(2)}) collective-permute-start(f32[2,512]{1,0:T(2,128)S(1)} %get-tuple-element.50), channel_id=1, source_target_pairs={{2,1},{4,3},{6,5},{8,7},{10,9},{12,11},{14,13},{16,15},{18,17},{20... | collective-permute-start | bytes 12296 | tf_op jit(solution)/shard_map/ppermute | solution.py:1139
